TPU v7x, 8 devices: a whole 2x2x1 slice. The times are simulated.
8 devices in a mesh: dp: 1 (over z), tp: 2 (over y), fsdp: 4 (over x, core).
Axes of the slice: x: 2, y: 2, z: 1, core: 2. Of those that a mesh axis runs over, the one named last changes fastest.
Arguments:
- x_in: bfloat16 [4, 2048, 4096], P(('dp', 'fsdp'))
- g_attn: bfloat16 [2, 4096], P(None, 'fsdp')
- w_q: bfloat16 [2, 4096, 4096], P(None, 'fsdp', 'tp')
- w_k: bfloat16 [2, 4096, 1024], P(None, 'fsdp', 'tp')
- w_v: bfloat16 [2, 4096, 1024], P(None, 'fsdp', 'tp')
- w_o: bfloat16 [2, 4096, 4096], P(None, 'tp', 'fsdp')
- g_mlp: bfloat16 [2, 4096], P(None, 'fsdp')
- w_gate: bfloat16 [2, 4096, 12288], P(None, 'fsdp', 'tp')
- w_up: bfloat16 [2, 4096, 12288], P(None, 'fsdp', 'tp')
- w_down: bfloat16 [2, 12288, 4096], P(None, 'tp', 'fsdp')
Outputs:
- output 1: bfloat16 [4, 2048, 4096], P(('dp', 'fsdp'))
- output 2: bfloat16 [2, 4, 2048, 1024], P(None, ('dp', 'fsdp'), None, 'tp')
- output 3: bfloat16 [2, 4, 2048, 1024], P(None, ('dp', 'fsdp'), None, 'tp')
All inputs are finite; a program needn't handle non-finite values.
Results may differ from a plain program's by a relative error of at most 0.02.
Values are sent between devices in bfloat16 or wider.
A program may use at most 1 GiB of HBM per device.

v0:
```python
import jax
import jax.numpy as jnp
from jax import lax
from jax.sharding import PartitionSpec as P

HEAD_DIM = 128
ROPE_THETA = 1.0e6
NORM_EPS = 1.0e-5
Q_BLOCK = 512


def rope_tables(seq_len):
    inv_freq = ROPE_THETA ** (-2.0 * jnp.arange(HEAD_DIM // 2, dtype=jnp.float32) / HEAD_DIM)
    angles = jnp.arange(seq_len, dtype=jnp.float32)[:, None] * inv_freq[None, :]
    return jnp.cos(angles), jnp.sin(angles)


def apply_rope(t_lin, cos_t, sin_t):
    half_dim = t_lin.shape[-1] // 2
    first_half = t_lin[..., :half_dim]
    second_half = t_lin[..., half_dim:]
    cos_b = cos_t[:, None, :]
    sin_b = sin_t[:, None, :]
    return jnp.concatenate([first_half * cos_b - second_half * sin_b, second_half * cos_b + first_half * sin_b], axis=-1)


def rms_norm(x_in, gain_vec):
    x_f32 = x_in.astype(jnp.float32)
    inv_rms = lax.rsqrt(jnp.mean(x_f32 * x_f32, axis=-1, keepdims=True) + NORM_EPS)
    return (x_f32 * inv_rms * gain_vec.astype(jnp.float32)).astype(jnp.bfloat16)


def causal_attention(q_rot, k_rot, v_val):
    n_batch, seq_len, kv_heads, q_group = q_rot.shape[0], q_rot.shape[1], q_rot.shape[2], q_rot.shape[3]
    blk_len = min(seq_len, Q_BLOCK)
    attn_scale = HEAD_DIM ** -0.5
    ctx_blocks = []
    for q_start in range(0, seq_len, blk_len):
        q_stop = q_start + blk_len
        scores = jnp.einsum('bqkgd,bskd->bkgqs', q_rot[:, q_start:q_stop], k_rot[:, :q_stop], preferred_element_type=jnp.float32) * attn_scale
        causal_mask = jnp.arange(q_stop)[None, :] <= (q_start + jnp.arange(blk_len))[:, None]
        scores = jnp.where(causal_mask, scores, -1.0e30)
        attn_probs = jax.nn.softmax(scores, axis=-1).astype(jnp.bfloat16)
        ctx_block = jnp.einsum('bkgqs,bskd->bqkgd', attn_probs, v_val[:, :q_stop], preferred_element_type=jnp.float32)
        ctx_blocks.append(ctx_block.astype(jnp.bfloat16))
    context = jnp.concatenate(ctx_blocks, axis=1)
    return context.reshape(n_batch, seq_len, kv_heads * q_group * HEAD_DIM)


def local_layer(x_loc, layer_w, cos_t, sin_t):
    g_attn, w_q, w_k, w_v, w_o, g_mlp, w_gate, w_up, w_down = layer_w
    n_batch = x_loc.shape[0]
    seq_len = x_loc.shape[1]
    q_heads = w_q.shape[1] // HEAD_DIM
    kv_heads = w_k.shape[1] // HEAD_DIM
    normed = rms_norm(x_loc, g_attn)
    q_lin = jnp.einsum('bsm,mn->bsn', normed, w_q, preferred_element_type=jnp.float32)
    k_lin = jnp.einsum('bsm,mn->bsn', normed, w_k, preferred_element_type=jnp.float32)
    v_val = jnp.einsum('bsm,mn->bsn', normed, w_v, preferred_element_type=jnp.float32).astype(jnp.bfloat16)
    q_rot = apply_rope(q_lin.reshape(n_batch, seq_len, q_heads, HEAD_DIM), cos_t, sin_t).astype(jnp.bfloat16)
    k_rot = apply_rope(k_lin.reshape(n_batch, seq_len, kv_heads, HEAD_DIM), cos_t, sin_t).astype(jnp.bfloat16)
    context = causal_attention(q_rot.reshape(n_batch, seq_len, kv_heads, q_heads // kv_heads, HEAD_DIM), k_rot, v_val.reshape(n_batch, seq_len, kv_heads, HEAD_DIM))
    attn_part = jnp.einsum('bsn,nm->bsm', context, w_o, preferred_element_type=jnp.float32).astype(jnp.bfloat16)
    attn_out = lax.psum(attn_part, 'tp')
    x_mid = (x_loc.astype(jnp.float32) + attn_out.astype(jnp.float32)).astype(jnp.bfloat16)
    normed_mlp = rms_norm(x_mid, g_mlp)
    gate_lin = jnp.einsum('bsm,mf->bsf', normed_mlp, w_gate, preferred_element_type=jnp.float32)
    up_lin = jnp.einsum('bsm,mf->bsf', normed_mlp, w_up, preferred_element_type=jnp.float32)
    hidden_act = (jax.nn.silu(gate_lin) * up_lin).astype(jnp.bfloat16)
    mlp_part = jnp.einsum('bsf,fm->bsm', hidden_act, w_down, preferred_element_type=jnp.float32).astype(jnp.bfloat16)
    mlp_out = lax.psum(mlp_part, 'tp')
    x_next = (x_mid.astype(jnp.float32) + mlp_out.astype(jnp.float32)).astype(jnp.bfloat16)
    return x_next, k_rot.reshape(n_batch, seq_len, kv_heads * HEAD_DIM), v_val


def solution(mesh):
    tok_spec = P(('dp', 'fsdp'), None, None)
    gain_spec = P(None, 'fsdp')
    col_spec = P(None, 'fsdp', 'tp')
    row_spec = P(None, 'tp', 'fsdp')
    cache_spec = P(None, ('dp', 'fsdp'), None, 'tp')

    def device_fn(x_loc, g_attn, w_q, w_k, w_v, w_o, g_mlp, w_gate, w_up, w_down):
        cos_t, sin_t = rope_tables(x_loc.shape[1])
        hidden = x_loc
        key_list = []
        value_list = []
        for layer_idx in range(w_q.shape[0]):
            layer_w = (
                lax.all_gather(g_attn[layer_idx], 'fsdp', axis=0, tiled=True),
                lax.all_gather(w_q[layer_idx], 'fsdp', axis=0, tiled=True),
                lax.all_gather(w_k[layer_idx], 'fsdp', axis=0, tiled=True),
                lax.all_gather(w_v[layer_idx], 'fsdp', axis=0, tiled=True),
                lax.all_gather(w_o[layer_idx], 'fsdp', axis=1, tiled=True),
                lax.all_gather(g_mlp[layer_idx], 'fsdp', axis=0, tiled=True),
                lax.all_gather(w_gate[layer_idx], 'fsdp', axis=0, tiled=True),
                lax.all_gather(w_up[layer_idx], 'fsdp', axis=0, tiled=True),
                lax.all_gather(w_down[layer_idx], 'fsdp', axis=1, tiled=True),
            )
            hidden, k_cache, v_cache = local_layer(hidden, layer_w, cos_t, sin_t)
            key_list.append(k_cache)
            value_list.append(v_cache)
        return hidden, jnp.stack(key_list), jnp.stack(value_list)

    return jax.shard_map(device_fn, mesh=mesh, in_specs=(tok_spec, gain_spec, col_spec, col_spec, col_spec, row_spec, gain_spec, col_spec, col_spec, row_spec), out_specs=(tok_spec, cache_spec, cache_spec), check_vma=False)
```

profile of v0, /device:TPU:0, one launch (start us, length us, event | category | flops | bytes accessed | tf_op | source)
XLA Modules:
  0.0 4496.3 jit_solution(4257250950218758434)
XLA Ops:
  78.2 15.1 fusion.110
  93.3 91.2 %all-gather.37.cloned.1.call-done = bf16[1,4096,2048]{2,1,0:T(8,128)(2,1)} async-done(((bf16[1,1024,2048]{2,1,0:T(8,128)(2,1)}), bf16[1,4096,2048]{2,1,0:T(8,128)(2,1)}) %all-gather.37.cloned.1.call-update) | async-done | bytes 16777232 | tf_op jit(solution)/shard_map/all_gather | solution.py:91
  184.6 21.2 copy.14
  205.7 43.4 fusion.92
  288.4 16.3 fusion.42
  304.7 22.4 fusion.18
  360.3 21.2 fusion.16
  381.6 27.3 fusion.2
  408.9 21.6 fusion
  430.4 16.6 convert_bitcast_fusion.10
  447.0 22.1 convert_bitcast_fusion.9
  469.1 28.4 convert_bitcast_fusion.8
  504.2 42.2 convert_bitcast_fusion.3
  546.5 17.8 fusion.205
  564.4 17.9 fusion.204
  582.3 17.4 fusion.203
  608.7 310.1 %all-reduce.5.cloned.1.call-done = bf16[1,2048,4096]{2,1,0:T(8,128)(2,1)} async-done(((bf16[1,2048,4096]{2,1,0:T(8,128)(2,1)}), bf16[1,2048,4096]{2,1,0:T(8,128)(2,1)}) %all-reduce.5.cloned.1.call-update) | async-done | bytes 16777232 | tf_op jit(solution)/shard_map/psum | solution.py:64
  918.7 20.4 fusion.24
  939.1 275.9 %all-gather.41.cloned.1.call-done = bf16[1,4096,6144]{2,1,0:T(8,128)(2,1)} async-done(((bf16[1,1024,6144]{2,1,0:T(8,128)(2,1)}), bf16[1,4096,6144]{2,1,0:T(8,128)(2,1)}) %all-gather.41.cloned.1.call-update) | async-done | bytes 50331664 | tf_op jit(solution)/shard_map/all_gather | solution.py:96
  1215.0 114.3 %fusion.14 = f32[2048,6144]{1,0:T(8,128)} fusion(bf16[1,4096,6144]{2,1,0:T(8,128)(2,1)} %all-gather.41.cloned.1.call-done, bf16[1,2048,4096]{2,1,0:T(8,128)(2,1)} %get-tuple-element.9, f32[4096]{0:T(1024)S(1)} %bitcast.542, f32[2048]{0:T(1024)S(1)} %add_rsqrt_fusion.2), kind=kOutput, calls=%fused_computation.22 | convolution fusion | flops 103112769536 | bytes 117465088 | tf_op jit(solution)/shard_map/bsm,mf->bsf/dot_general | solution.py:67
  1329.3 181.8 %all-gather.43.cloned.1.call-done = bf16[1,4096,6144]{2,1,0:T(8,128)(2,1)} async-done(((bf16[1,1024,6144]{2,1,0:T(8,128)(2,1)}), bf16[1,4096,6144]{2,1,0:T(8,128)(2,1)}) %all-gather.43.cloned.1.call-update) | async-done | bytes 50331664 | tf_op jit(solution)/shard_map/all_gather | solution.py:97
  1511.1 127.0 %multiply_convert_fusion.1 = bf16[2048,6144]{1,0:T(8,128)(2,1)} fusion(f32[2048,6144]{1,0:T(8,128)} %fusion.14, bf16[1,4096,6144]{2,1,0:T(8,128)(2,1)} %all-gather.43.cloned.1.call-done, bf16[1,2048,4096]{2,1,0:T(8,128)(2,1)} %get-tuple-element.9, f32[4096]{0:T(1024)S(1)} %bitcast.543, f32[2048]{0:T(1024)S(1)} %add_rsqrt_fusion.2), kind=kOutput, calls=%fused_computation.33 | convolution fusion | flops 103188267008 | bytes 142630912 | tf_op jit(solution)/shard_map/bsm,mf->bsf/dot_general | solution.py:68
  1638.1 169.1 %all-gather.45.cloned.1.call-done = bf16[1,6144,4096]{2,1,0:T(8,128)(2,1)} async-done(((bf16[1,6144,1024]{2,1,0:T(8,128)(2,1)}), bf16[1,6144,4096]{2,1,0:T(8,128)(2,1)}) %all-gather.45.cloned.1.call-update) | async-done | bytes 50331664 | tf_op jit(solution)/shard_map/all_gather | solution.py:98
  1807.2 117.6 %convert_bitcast_fusion.2 = bf16[1,2048,4096]{2,1,0:T(8,128)(2,1)} fusion(bf16[2048,6144]{1,0:T(8,128)(2,1)} %multiply_convert_fusion.1, bf16[1,6144,4096]{2,1,0:T(8,128)(2,1)} %all-gather.45.cloned.1.call-done), kind=kOutput, calls=%fused_computation.108 | convolution fusion | flops 103087603712 | bytes 92274688 | tf_op jit(solution)/shard_map/bsf,fm->bsm/dot_general | solution.py:70
  1946.9 21.4 copy.26
  1968.3 353.2 %all-reduce.7.cloned.1.call-done = bf16[1,2048,4096]{2,1,0:T(8,128)(2,1)} async-done(((bf16[1,2048,4096]{2,1,0:T(8,128)(2,1)}), bf16[1,2048,4096]{2,1,0:T(8,128)(2,1)}) %all-reduce.7.cloned.1.call-update) | async-done | bytes 16777232 | tf_op jit(solution)/shard_map/psum | solution.py:71
  2321.5 14.4 fusion.28
  2362.9 43.5 fusion.95
  2445.1 16.5 fusion.43
  2461.6 22.0 fusion.19
  2518.0 15.0 fusion.41
  2532.9 21.1 fusion.17
  2554.0 27.5 fusion.3
  2581.5 21.6 fusion.1
  2603.1 16.6 convert_bitcast_fusion.6
  2619.6 22.1 convert_bitcast_fusion.5
  2641.7 28.4 convert_bitcast_fusion.4
  2676.8 42.4 convert_bitcast_fusion.1
  2729.1 362.7 %all-reduce.9.cloned.1.call-done = bf16[1,2048,4096]{2,1,0:T(8,128)(2,1)} async-done(((bf16[1,2048,4096]{2,1,0:T(8,128)(2,1)}), bf16[1,2048,4096]{2,1,0:T(8,128)(2,1)}) %all-reduce.9.cloned.1.call-update) | async-done | bytes 16777232 | tf_op jit(solution)/shard_map/psum | solution.py:64
  3091.8 24.4 fusion.32
  3116.2 271.9 %all-gather.55.cloned.1.call-done = bf16[1,4096,6144]{2,1,0:T(8,128)(2,1)} async-done(((bf16[1,1024,6144]{2,1,0:T(8,128)(2,1)}), bf16[1,4096,6144]{2,1,0:T(8,128)(2,1)}) %all-gather.55.cloned.1.call-update) | async-done | bytes 50331664 | tf_op jit(solution)/shard_map/all_gather | solution.py:96
  3388.1 114.3 %fusion.8 = f32[2048,6144]{1,0:T(8,128)} fusion(bf16[1,4096,6144]{2,1,0:T(8,128)(2,1)} %all-gather.55.cloned.1.call-done, bf16[1,2048,4096]{2,1,0:T(8,128)(2,1)} %get-tuple-element.7, f32[4096]{0:T(1024)S(1)} %bitcast.540, f32[2048]{0:T(1024)S(1)} %add_rsqrt_fusion), kind=kOutput, calls=%fused_computation.16 | convolution fusion | flops 103112769536 | bytes 117465088 | tf_op jit(solution)/shard_map/bsm,mf->bsf/dot_general | solution.py:67
  3502.4 181.7 %all-gather.57.cloned.1.call-done = bf16[1,4096,6144]{2,1,0:T(8,128)(2,1)} async-done(((bf16[1,1024,6144]{2,1,0:T(8,128)(2,1)}), bf16[1,4096,6144]{2,1,0:T(8,128)(2,1)}) %all-gather.57.cloned.1.call-update) | async-done | bytes 50331664 | tf_op jit(solution)/shard_map/all_gather | solution.py:97
  3684.0 126.9 %multiply_convert_fusion = bf16[2048,6144]{1,0:T(8,128)(2,1)} fusion(f32[2048,6144]{1,0:T(8,128)} %fusion.8, bf16[1,4096,6144]{2,1,0:T(8,128)(2,1)} %all-gather.57.cloned.1.call-done, bf16[1,2048,4096]{2,1,0:T(8,128)(2,1)} %get-tuple-element.7, f32[4096]{0:T(1024)S(1)} %bitcast.541, f32[2048]{0:T(1024)S(1)} %add_rsqrt_fusion), kind=kOutput, calls=%fused_computation.24 | convolution fusion | flops 103188267008 | bytes 142630912 | tf_op jit(solution)/shard_map/bsm,mf->bsf/dot_general | solution.py:68
  3811.0 169.0 %all-gather.59.cloned.1.call-done = bf16[1,6144,4096]{2,1,0:T(8,128)(2,1)} async-done(((bf16[1,6144,1024]{2,1,0:T(8,128)(2,1)}), bf16[1,6144,4096]{2,1,0:T(8,128)(2,1)}) %all-gather.59.cloned.1.call-update) | async-done | bytes 50331664 | tf_op jit(solution)/shard_map/all_gather | solution.py:98
  3980.0 117.6 %convert_bitcast_fusion = bf16[1,2048,4096]{2,1,0:T(8,128)(2,1)} fusion(bf16[2048,6144]{1,0:T(8,128)(2,1)} %multiply_convert_fusion, bf16[1,6144,4096]{2,1,0:T(8,128)(2,1)} %all-gather.59.cloned.1.call-done), kind=kOutput, calls=%fused_computation.104 | convolution fusion | flops 103087603712 | bytes 92274688 | tf_op jit(solution)/shard_map/bsf,fm->bsm/dot_general | solution.py:70
  4120.6 349.3 %all-reduce.11.cloned.1.call-done = bf16[1,2048,4096]{2,1,0:T(8,128)(2,1)} async-done(((bf16[1,2048,4096]{2,1,0:T(8,128)(2,1)}), bf16[1,2048,4096]{2,1,0:T(8,128)(2,1)}) %all-reduce.11.cloned.1.call-update) | async-done | bytes 16777232 | tf_op jit(solution)/shard_map/psum | solution.py:71
  4469.9 19.3 fusion.35
  (176 shorter events, 320.4 us)
Async XLA Ops:
  7.2 44.1 all-gather.35.cloned.1.call-start
  10.2 68.0 %all-gather.33.cloned.1.call-start = ((), (), s32[]{:S(2)}) async-start(), calls=%async_computation.4 | async-start | bytes 5242880 | tf_op jit(solution)/shard_map/all_gather | solution.py:93
  13.3 171.3 %all-gather.37.cloned.1.call-start = ((), (), s32[]{:S(2)}) async-start(), calls=%async_computation.6 | async-start | bytes 20971520 | tf_op jit(solution)/shard_map/all_gather | solution.py:91
  19.5 7.0 copy-start.31
  19.5 484.7 %all-gather.39.cloned.1.call-start = ((), (), s32[]{:S(2)}) async-start(), calls=%async_computation.7 | async-start | bytes 20971520 | tf_op jit(solution)/shard_map/all_gather | solution.py:94
  25.6 893.1 %all-reduce.5.cloned.1.call-start = ((), (), s32[]{:S(2)}) async-start(), calls=%async_computation | async-start | bytes 33554432 | tf_op jit(solution)/shard_map/psum | solution.py:64
  46.7 202.5 %copy-start.11 = (f32[2048,64]{0,1:T(8,128)}, f32[2048,64]{0,1:T(8,128)S(1)}, u32[]{:S(2)}) copy-start(f32[2048,64]{0,1:T(8,128)S(1)} %get-tuple-element.36) | copy-start | bytes 1572868
  46.7 202.5 %copy-start.13 = (f32[2048,64]{0,1:T(8,128)}, f32[2048,64]{0,1:T(8,128)S(1)}, u32[]{:S(2)}) copy-start(f32[2048,64]{0,1:T(8,128)S(1)} %get-tuple-element.37) | copy-start | bytes 1572868
  258.7 16.8 copy-start.15
  275.5 12.9 copy-start
  275.5 12.9 copy-start.6
  288.4 16.4 copy-start.4
  360.3 21.3 copy-start.2
  360.3 21.3 copy-start.18
  360.3 21.3 copy-start.20
  447.0 22.1 copy-start.25
  469.1 28.4 copy-start.29
  546.5 668.6 %all-gather.41.cloned.1.call-start = ((), (), s32[]{:S(2)}) async-start(), calls=%async_computation.8 | async-start | bytes 62914560 | tf_op jit(solution)/shard_map/all_gather | solution.py:96
  564.3 946.8 %all-gather.43.cloned.1.call-start = ((), (), s32[]{:S(2)}) async-start(), calls=%async_computation.9 | async-start | bytes 62914560 | tf_op jit(solution)/shard_map/all_gather | solution.py:97
  582.2 1224.9 %all-gather.45.cloned.1.call-start = ((), (), s32[]{:S(2)}) async-start(), calls=%async_computation.10 | async-start | bytes 62914560 | tf_op jit(solution)/shard_map/all_gather | solution.py:98
  599.7 1334.0 %all-gather.49.cloned.1.call-start = ((), (), s32[]{:S(2)}) async-start(), calls=%async_computation.12 | async-start | bytes 5242880 | tf_op jit(solution)/shard_map/all_gather | solution.py:92
  600.4 1346.4 %all-gather.51.cloned.1.call-start = ((), (), s32[]{:S(2)}) async-start(), calls=%async_computation.13 | async-start | bytes 20971520 | tf_op jit(solution)/shard_map/all_gather | solution.py:91
  601.0 1720.5 %all-reduce.7.cloned.1.call-start = ((), (), s32[]{:S(2)}) async-start(), calls=%async_computation.1 | async-start | bytes 33554432 | tf_op jit(solution)/shard_map/psum | solution.py:71
  1924.8 568.1 %all-gather.47.cloned.1.call-start = ((), (), s32[]{:S(2)}) async-start(), calls=%async_computation.11 | async-start | bytes 5242880 | tf_op jit(solution)/shard_map/all_gather | solution.py:93
  1925.4 751.4 %all-gather.53.cloned.1.call-start = ((), (), s32[]{:S(2)}) async-start(), calls=%async_computation.14 | async-start | bytes 20971520 | tf_op jit(solution)/shard_map/all_gather | solution.py:94
  1926.1 1165.7 %all-reduce.9.cloned.1.call-start = ((), (), s32[]{:S(2)}) async-start(), calls=%async_computation.2 | async-start | bytes 33554432 | tf_op jit(solution)/shard_map/psum | solution.py:64
  2321.5 15.5 copy-start.1
  2337.1 12.5 copy-start.24
  2349.6 10.4 copy-start.10
  2349.6 10.4 copy-start.12
  2349.6 10.4 copy-start.14
  2362.9 69.6 %copy-start.21 = (bf16[1,2048,4,64]{1,3,2,0:T(8,128)(2,1)}, bf16[1,2048,4,64]{1,3,2,0:T(8,128)(2,1)S(1)}, u32[]{:S(2)}) copy-start(bf16[1,2048,4,64]{1,3,2,0:T(8,128)(2,1)S(1)} %get-tuple-element.25) | copy-start | bytes 3145732
  2415.7 18.3 copy-start.16
  2432.5 12.6 slice-start
  2434.0 11.1 slice-start.1
  2434.0 11.1 copy-start.7
  2445.1 16.5 copy-start.5
  2507.0 11.0 copy-start.26
  2532.9 21.1 copy-start.3
  2532.9 21.1 copy-start.22
  2581.5 21.6 copy-start.30
  2619.6 22.1 copy-start.27
  2641.7 28.4 copy-start.28
  2719.2 668.9 %all-gather.55.cloned.1.call-start = ((), (), s32[]{:S(2)}) async-start(), calls=%async_computation.15 | async-start | bytes 62914560 | tf_op jit(solution)/shard_map/all_gather | solution.py:96
  2719.8 964.3 %all-gather.57.cloned.1.call-start = ((), (), s32[]{:S(2)}) async-start(), calls=%async_computation.16 | async-start | bytes 62914560 | tf_op jit(solution)/shard_map/all_gather | solution.py:97
  2720.4 1259.6 %all-gather.59.cloned.1.call-start = ((), (), s32[]{:S(2)}) async-start(), calls=%async_computation.17 | async-start | bytes 62914560 | tf_op jit(solution)/shard_map/all_gather | solution.py:98
  2720.9 1749.0 %all-reduce.11.cloned.1.call-start = ((), (), s32[]{:S(2)}) async-start(), calls=%async_computation.3 | async-start | bytes 33554432 | tf_op jit(solution)/shard_map/psum | solution.py:71
  4101.7 14.9 copy-start.23
  (7 other events, 9.8 us)
Sparse Core Ops, SparseCore 0:
  10.3 34.7 all-gather.34
  46.7 31.4 all-gather.32
  80.3 104.1 all-gather.36
  185.9 104.1 all-gather.38
  546.6 372.1 all-reduce.4
  920.1 294.8 all-gather.40
  1216.6 294.5 all-gather.42
  1512.6 294.4 all-gather.44
  1808.7 31.4 all-gather.48
  1842.2 104.6 all-gather.50
  1949.3 372.1 all-reduce.6
  2322.9 31.8 all-gather.46
  2356.3 104.1 all-gather.52
  2719.3 372.4 all-reduce.8
  3093.2 294.8 all-gather.54
  3389.5 294.4 all-gather.56
  3685.4 294.4 all-gather.58
  4097.7 372.1 all-reduce.10
where the time goes:
time: 4510 us; the launch traced here: 4500 us
  waiting for transfers between devices  2730 us (61%)
  matrix products  1250 us (28%)
  other arithmetic  285 us (6%)
  local copies, waits for them, and re-layouts  180 us (4%)
    psum x2, waiting for transfers between devices, local_layer(): mlp_out = lax.psum(mlp_part, 'tp')  703 us
    psum x2, waiting for transfers between devices, local_layer(): attn_out = lax.psum(attn_part, 'tp')  673 us
    all_gather x2, waiting for transfers between devices, device_fn(): lax.all_gather(w_gate[layer_idx], 'fsdp', axis=0, tiled=True)  548 us
    all_gather x2, waiting for transfers between devices, device_fn(): lax.all_gather(w_up[layer_idx], 'fsdp', axis=0, tiled=True)  363 us
    all_gather x2, waiting for transfers between devices, device_fn(): lax.all_gather(w_down[layer_idx], 'fsdp', axis=1, tiled=True)  338 us
    dot_general x2, matrix products, local_layer(): jnp.einsum('bsm,mf->bsf', normed_mlp, w_up, preferred_element_type=jnp.fl...  254 us
    dot_general x2, matrix products, local_layer(): jnp.einsum('bsf,fm->bsm', hidden_act, w_down, preferred_element_type=jnp....  235 us
    dot_general x2, matrix products, local_layer(): jnp.einsum('bsm,mf->bsf', normed_mlp, w_gate, preferred_element_type=jnp....  229 us
  transfers between devices with their start and end apart: 18, of which 13 were waited for; matrix products, arithmetic and copies ran while one was open for 33% of the time, Pallas kernels for 0%

commit v1 on v0

v1 whole, which is shorter than its diff:
```python
import functools

import jax
import jax.numpy as jnp
from jax import lax
from jax.experimental import pallas as pl
from jax.experimental.pallas import tpu as pltpu
from jax.sharding import PartitionSpec as P


HEAD_DIM = 128
ROPE_THETA = 1.0e6
NORM_EPS = 1.0e-5
LOG2E = 1.4426950408889634
GU_BLOCKS = (7, 7, 6, 4)
GU_BN = 256

X, C, N, Y, K = "x", "c", "n", "y", "K"
G, Q, KV, O, GU, D, GATE, UP, DOWN = "g", "q", "kv", "o", "gu", "d", "gate", "up", "down"
I0, I1, I2, I3 = range(4)
FIRST, QKV, ATTN, OA, OB, ADDO, DA, DC, ADDM, LAST = "first", "qkv", "attn", "oa", "ob", "addo", "da", "dc", "addm", "last"

PLAN = (
    (X, Q, I0), (N, Q, I0), (X, G), (N, G), (X, KV, I0), (N, KV, I0), (X, O, I0), (C, G), (X, GU, I0, I0),
    (X, GU, I0, I1), (N, O),
    (K, FIRST, I0), (K, FIRST, I1),
    (C, Q, I0), (C, KV, I0), (X, GU, I0, I2),
    (K, QKV, I0, I0), (K, ATTN, I0, I0),
    (C, O, I0), (X, GU, I0, I3), (N, GATE), (N, UP),
    (K, OA, I0, I0), (Y, OA, I0, I0), (K, OB, I0, I0), (Y, OB, I0, I0), (K, QKV, I0, I1), (K, ATTN, I0, I1), (K, OA, I0, I1),
    (Y, OA, I0, I1), (K, OB, I0, I1), (Y, OB, I0, I1),
    (C, GU, I0, I0), (X, D, I0, I0), (N, DOWN),
    (K, ADDO, I0, I0), (K, GU, I0, I0, I0),
    (C, GU, I0, I1), (X, D, I0, I1),
    (K, GU, I0, I1, I0), (K, ADDO, I0, I1), (K, GU, I0, I0, I1),
    (C, GU, I0, I2), (X, Q, I1), (X, KV, I1),
    (K, GU, I0, I1, I1), (K, GU, I0, I2, I0),
    (C, GU, I0, I3), (X, O, I1), (N, Q, I1), (N, KV, I1),
    (K, GU, I0, I2, I1), (K, GU, I0, I3, I0), (K, DA, I0, I0), (Y, DA, I0, I0), (K, DC, I0, I0), (Y, DC, I0, I0),
    (K, GU, I0, I3, I1),
    (K, DA, I0, I1), (Y, DA, I0, I1),
    (C, D, I0, I0), (X, GU, I1, I0),
    (K, DC, I0, I1), (Y, DC, I0, I1), (K, D, I0, I0, I0), (Y, D, I0, I0, I0),
    (C, D, I0, I1), (X, GU, I1, I1),
    (K, D, I1, I0, I0), (Y, D, I1, I0, I0), (K, D, I0, I0, I1), (Y, D, I0, I0, I1), (K, D, I1, I0, I1),
    (Y, D, I1, I0, I1), (K, ADDM, I0, I0),
    (C, Q, I1), (C, KV, I1), (X, GU, I1, I2),
    (K, QKV, I1, I0), (K, ATTN, I1, I0), (K, OA, I1, I0), (Y, OA, I1, I0),
    (C, O, I1), (X, GU, I1, I3),
    (K, ADDM, I0, I1), (K, OB, I1, I0), (Y, OB, I1, I0), (K, QKV, I1, I1), (K, ATTN, I1, I1), (K, OA, I1, I1),
    (Y, OA, I1, I1),
    (K, OB, I1, I1), (Y, OB, I1, I1),
    (C, GU, I1, I0), (X, D, I1, I0),
    (K, ADDO, I1, I0), (K, GU, I1, I0, I0),
    (C, GU, I1, I1), (X, D, I1, I1),
    (K, GU, I1, I1, I0), (K, ADDO, I1, I1), (K, GU, I1, I0, I1), (K, GU, I1, I1, I1),
    (C, GU, I1, I2),
    (K, GU, I1, I2, I0), (K, GU, I1, I2, I1),
    (C, GU, I1, I3),
    (K, GU, I1, I3, I0), (K, DA, I1, I0), (Y, DA, I1, I0), (K, DC, I1, I0), (Y, DC, I1, I0), (K, GU, I1, I3, I1),
    (K, DA, I1, I1),
    (Y, DA, I1, I1), (K, DC, I1, I1), (Y, DC, I1, I1),
    (C, D, I1, I0),
    (K, D, I0, I1, I0), (Y, D, I0, I1, I0), (K, D, I0, I1, I1), (Y, D, I0, I1, I1),
    (C, D, I1, I1),
    (K, D, I1, I1, I0), (Y, D, I1, I1, I0), (K, D, I1, I1, I1), (Y, D, I1, I1, I1),
    (K, LAST, I0, I0), (K, LAST, I0, I1), (K, LAST, I1, I0), (K, LAST, I1, I1), (K, LAST, I2, I0), (K, LAST, I2, I1),
    (K, LAST, I3, I0),
    (K, LAST, I3, I1),
)

VMEM_BYTES = 62 * 1024 * 1024

F32 = jnp.float32
BF16 = jnp.bfloat16
ANY = pl.BlockSpec(memory_space=pl.ANY)


def name_of(op, *idx):
    return op + "".join(map(str, idx))


def rope_tables(seq_len):
    inv_freq = ROPE_THETA ** (-2.0 * jnp.arange(HEAD_DIM // 2, dtype=F32) / HEAD_DIM)
    angles = jnp.arange(seq_len, dtype=F32)[:, None] * inv_freq[None, :]
    cos_t, sin_t = jnp.cos(angles), jnp.sin(angles)
    return jnp.concatenate([cos_t, cos_t], axis=1), jnp.concatenate([-sin_t, sin_t], axis=1)


def params(flops_grid=1):
    return pltpu.CompilerParams(dimension_semantics=("arbitrary",) * flops_grid, vmem_limit_bytes=VMEM_BYTES)


def cost(flops, nbytes, trans=0):
    return pl.CostEstimate(flops=int(flops), bytes_accessed=int(nbytes), transcendentals=int(trans))


def left_rows(a_hbm, a_ref, a_sem, tm):
    def copy(m):
        r = pl.ds(pl.multiple_of(m * tm, tm), tm)
        return pltpu.make_async_copy(a_hbm.at[r, :], a_ref.at[r, :], a_sem.at[m])

    def start():
        for m in range(a_hbm.shape[0] // tm):
            copy(m).start()

    def wait(m):
        @pl.when(pl.program_id(0) == 0)
        def _():
            copy(m).wait()

    return start, wait


def qkv_body(a_hbm, cos_ref, sin_ref, *refs, bn, n_rope, tm):
    qs, kvs = refs[:4], refs[4:8]
    o_ref, buf, sem, a_ref, a_sem = refs[8:]
    n = pl.program_id(0)
    a_start, a_wait = left_rows(a_hbm, a_ref, a_sem, tm)
    depth = qs[0].shape[0]
    n_q = qs[0].shape[1] // bn

    def copies(ws, blk, slot):
        cols = pl.ds(pl.multiple_of(blk * bn, bn), bn)
        return [pltpu.make_async_copy(w.at[:, cols], buf.at[slot, pl.ds(i * depth, depth), :], sem.at[slot])
                for i, w in enumerate(ws)]

    @pl.when(n == 0)
    def _():
        for cp in copies(qs, 0, 0):
            cp.start()
        a_start()

    @pl.when(n + 1 < n_q)
    def _():
        for cp in copies(qs, n + 1, (n + 1) % 2):
            cp.start()

    @pl.when((n + 1 >= n_q) & (n + 1 < pl.num_programs(0)))
    def _():
        for cp in copies(kvs, n + 1 - n_q, (n + 1) % 2):
            cp.start()

    slot = n % 2
    for cp in copies(qs, 0, slot):
        cp.wait()

    def rows(m, _):
        r = pl.ds(pl.multiple_of(m * tm, tm), tm)
        a_wait(m)
        acc = jnp.dot(a_ref[r, :], buf[slot], preferred_element_type=F32)

        @pl.when(n < n_rope)
        def _():
            cos_b, sin_b = cos_ref[r, :], sin_ref[r, :]
            for h in range(bn // HEAD_DIM):
                part = acc[:, h * HEAD_DIM:(h + 1) * HEAD_DIM]
                turned = pltpu.roll(part, HEAD_DIM // 2, 1)
                o_ref[r, h * HEAD_DIM:(h + 1) * HEAD_DIM] = (part * cos_b + turned * sin_b).astype(BF16)

        @pl.when(n >= n_rope)
        def _():
            o_ref[r, :] = acc.astype(BF16)

        return 0

    lax.fori_loop(0, a_ref.shape[0] // tm, rows, 0)


def qkv_call(a, cos_t, sin_t, qs, kvs, rope_cols):
    t, k = a.shape
    n_all = qs[0].shape[1] + kvs[0].shape[1]
    bn, tm = 512, 512
    return pl.pallas_call(
        functools.partial(qkv_body, bn=bn, n_rope=rope_cols // bn, tm=tm),
        out_shape=jax.ShapeDtypeStruct((t, n_all), BF16),
        grid=(n_all // bn,),
        in_specs=[ANY, pl.BlockSpec((t, HEAD_DIM), lambda n: (0, 0)),
                  pl.BlockSpec((t, HEAD_DIM), lambda n: (0, 0))] + [ANY] * 8,
        out_specs=pl.BlockSpec((t, bn), lambda n: (0, n)),
        scratch_shapes=[pltpu.VMEM((2, k, bn), BF16), pltpu.SemaphoreType.DMA((2,)),
                        pltpu.VMEM((t, k), BF16), pltpu.SemaphoreType.DMA((t // tm,))],
        compiler_params=params(),
        cost_estimate=cost(2 * t * k * n_all, 2 * (t * k + k * n_all + t * n_all)),
    )(a, cos_t, sin_t, *qs, *kvs)


def gu_body(*refs, bn, base, tm, layer, aliased):
    a_hbm, g0, u0, g1, u1, c2, c3 = refs[:7]
    o_ref, gbuf, ubuf, sem, a_ref, a_sem = refs[7 + aliased:]
    n = pl.program_id(0)
    a_start, a_wait = left_rows(a_hbm, a_ref, a_sem, tm)
    nb = pl.num_programs(0)
    depth = c2.shape[0]
    half = c2.shape[1] // 2

    def copies(blk, slot):
        own = pl.ds(pl.multiple_of(base + blk * bn, bn), bn)
        gcol = pl.ds(pl.multiple_of(blk * bn, bn), bn)
        ucol = pl.ds(pl.multiple_of(half + blk * bn, bn), bn)
        srcs = [(g0.at[layer, :, own], u0.at[layer, :, own]), (g1.at[layer, :, own], u1.at[layer, :, own]),
                (c2.at[:, gcol], c2.at[:, ucol]), (c3.at[:, gcol], c3.at[:, ucol])]
        out = []
        for i, (gs, us) in enumerate(srcs):
            rows = pl.ds(i * depth, depth)
            out.append(pltpu.make_async_copy(gs, gbuf.at[slot, rows, :], sem.at[slot]))
            out.append(pltpu.make_async_copy(us, ubuf.at[slot, rows, :], sem.at[slot]))
        return out

    @pl.when(n == 0)
    def _():
        for cp in copies(0, 0):
            cp.start()
        a_start()

    @pl.when(n + 1 < nb)
    def _():
        for cp in copies(n + 1, (n + 1) % 2):
            cp.start()

    slot = n % 2
    for cp in copies(n, slot):
        cp.wait()

    def rows(m, _):
        r = pl.ds(pl.multiple_of(m * tm, tm), tm)
        a_wait(m)
        gate = jnp.dot(a_ref[r, :], gbuf[slot], preferred_element_type=F32)
        up = jnp.dot(a_ref[r, :], ubuf[slot], preferred_element_type=F32)
        o_ref[r, :] = (gate * jax.nn.sigmoid(gate) * up).astype(BF16)
        return 0

    lax.fori_loop(0, a_ref.shape[0] // tm, rows, 0)


def gu_call(a, g_own, u_own, g_core, u_core, c2, c3, u_prev, first, layer, f_loc):
    t, k = a.shape
    width = c2.shape[1] // 2
    bn, tm = GU_BN, 512
    nb = width // bn
    aliased = u_prev is not None
    args = [a, g_own, u_own, g_core, u_core, c2, c3] + ([u_prev] if aliased else [])
    return pl.pallas_call(
        functools.partial(gu_body, bn=bn, base=first * bn, tm=tm, layer=layer, aliased=int(aliased)),
        out_shape=jax.ShapeDtypeStruct((t, f_loc), BF16),
        grid=(nb,),
        in_specs=[ANY] * len(args),
        out_specs=pl.BlockSpec((t, bn), lambda n: (0, first + n)),
        scratch_shapes=[pltpu.VMEM((2, k, bn), BF16), pltpu.VMEM((2, k, bn), BF16), pltpu.SemaphoreType.DMA((2,)),
                        pltpu.VMEM((t, k), BF16), pltpu.SemaphoreType.DMA((t // tm,))],
        input_output_aliases={7: 0} if aliased else {},
        compiler_params=params(),
        cost_estimate=cost(4 * t * k * width, 2 * (t * k + 2 * k * width + t * width)),
    )(*args)


def cols_body(*refs, plan, n_w, tm):
    ws = refs[1:1 + n_w]
    o_ref, buf, sem, a_ref, a_sem = refs[1 + n_w:]
    n = pl.program_id(0)
    a_start, a_wait = left_rows(refs[0], a_ref, a_sem, tm)
    bw = buf.shape[2]

    def src(j):
        w, layer, col = plan[j]
        ref = ws[w]
        return ref.at[:, pl.ds(col, bw)] if layer is None else ref.at[layer, :, pl.ds(col, bw)]

    @pl.when(n == 0)
    def _():
        pltpu.make_async_copy(src(0), buf.at[0], sem.at[0]).start()
        a_start()

    for j in range(1, len(plan)):
        @pl.when(n + 1 == j)
        def _(j=j):
            pltpu.make_async_copy(src(j), buf.at[j % 2], sem.at[j % 2]).start()

    slot = n % 2
    pltpu.make_async_copy(src(0), buf.at[slot], sem.at[slot]).wait()

    def rows(m, _):
        r = pl.ds(pl.multiple_of(m * tm, tm), tm)
        a_wait(m)
        o_ref[r, :] = jnp.dot(a_ref[r, :], buf[slot], preferred_element_type=F32).astype(BF16)
        return 0

    lax.fori_loop(0, a_ref.shape[0] // tm, rows, 0)


def cols_call(a, ws, plan, bw):
    t, k = a.shape
    tm = 512
    width = bw * len(plan)
    return pl.pallas_call(
        functools.partial(cols_body, plan=plan, n_w=len(ws), tm=tm),
        out_shape=jax.ShapeDtypeStruct((t, width), BF16),
        grid=(len(plan),),
        in_specs=[ANY] * (1 + len(ws)),
        out_specs=pl.BlockSpec((t, bw), lambda n: (0, n)),
        scratch_shapes=[pltpu.VMEM((2, k, bw), BF16), pltpu.SemaphoreType.DMA((2,)),
                        pltpu.VMEM((t, k), BF16), pltpu.SemaphoreType.DMA((t // tm,))],
        compiler_params=params(),
        cost_estimate=cost(2 * t * k * width, 2 * (t * k + k * width + t * width)),
    )(a, *ws)


def attn_body(q_ref, *refs, n_past, bq, scale2):
    past_k = refs[:n_past]
    k_ref = refs[n_past]
    past_v = refs[n_past + 1:2 * n_past + 1]
    v_ref = refs[2 * n_past + 1]
    o_ref = refs[2 * n_past + 2]
    nt = (((1,), (1,)), ((), ()))
    for blk in range(q_ref.shape[0] // bq):
        lo = blk * bq
        q = q_ref[lo:lo + bq, :]
        keys = [r[...] for r in past_k] + ([k_ref[:lo, :]] if lo else [])
        vals = [r[...] for r in past_v] + ([v_ref[:lo, :]] if lo else [])
        scores = [lax.dot_general(q, kk, nt, preferred_element_type=F32) for kk in keys]
        diag = lax.dot_general(q, k_ref[lo:lo + bq, :], nt, preferred_element_type=F32)
        row = lax.broadcasted_iota(jnp.int32, (bq, bq), 0)
        col = lax.broadcasted_iota(jnp.int32, (bq, bq), 1)
        scores.append(jnp.where(col <= row, diag, -1.0e30))
        vals.append(v_ref[lo:lo + bq, :])
        top = jnp.max(scores[0], axis=1, keepdims=True)
        for s in scores[1:]:
            top = jnp.maximum(top, jnp.max(s, axis=1, keepdims=True))
        probs = [jnp.exp2((s - top) * scale2) for s in scores]
        total = jnp.sum(probs[0], axis=1, keepdims=True)
        for p in probs[1:]:
            total = total + jnp.sum(p, axis=1, keepdims=True)
        inv = 1.0 / total
        ctx = None
        for p, vv in zip(probs, vals):
            part = jnp.dot((p * inv).astype(BF16), vv, preferred_element_type=F32)
            ctx = part if ctx is None else ctx + part
        o_ref[lo:lo + bq, :] = ctx.astype(BF16)


def attn_call(qkv, past, n_q, n_kv):
    t = qkv.shape[0]
    group = n_q // n_kv

    def k_spec(arr):
        return pl.BlockSpec((arr.shape[0], HEAD_DIM), lambda h: (0, n_q + h // group))

    def v_spec(arr):
        return pl.BlockSpec((arr.shape[0], HEAD_DIM), lambda h: (0, n_q + n_kv + h // group))

    arrs = list(past) + [qkv]
    seen = sum(p.shape[0] for p in past) * t + t * t // 2
    return pl.pallas_call(
        functools.partial(attn_body, n_past=len(past), bq=256, scale2=HEAD_DIM ** -0.5 * LOG2E),
        out_shape=jax.ShapeDtypeStruct((t, n_q * HEAD_DIM), BF16),
        grid=(n_q,),
        in_specs=[pl.BlockSpec((t, HEAD_DIM), lambda h: (0, h))] + [k_spec(a) for a in arrs] + [v_spec(a) for a in arrs],
        out_specs=pl.BlockSpec((t, HEAD_DIM), lambda h: (0, h)),
        compiler_params=params(),
        cost_estimate=cost(4 * 4 * n_q * seen * HEAD_DIM, 2 * 2 * t * n_q * HEAD_DIM, n_q * seen),
    )(qkv, *arrs, *arrs)


def norm_rows(x, g_row):
    xf = x.astype(F32)
    inv = lax.rsqrt(jnp.mean(xf * xf, axis=-1, keepdims=True) + NORM_EPS)
    return (xf * inv * g_row).astype(BF16)


def first_body(_, x0, x1, x2, x3, g_ref, xp_ref, h_ref):
    x = jnp.concatenate([r[...] for r in (x0, x1, x2, x3)], axis=1)
    xp_ref[...] = x
    h_ref[...] = norm_rows(x, g_ref[...])


def first_call(x, order, g, row0, t):
    d = x.shape[1]
    q = d // 4
    tb = 128
    blk = [pl.BlockSpec((tb, q), lambda r, o, i=i: (row0 // tb + r, o[i])) for i in range(4)]
    row = pl.BlockSpec((tb, d), lambda r, o: (r, 0))
    return pl.pallas_call(
        first_body,
        grid_spec=pltpu.PrefetchScalarGridSpec(
            num_scalar_prefetch=1, grid=(t // tb,),
            in_specs=blk + [pl.BlockSpec((1, d), lambda r, o: (0, 0))], out_specs=[row, row]),
        out_shape=[jax.ShapeDtypeStruct((t, d), BF16)] * 2,
        compiler_params=params(), cost_estimate=cost(10 * t * d, 6 * t * d),
    )(order, x, x, x, x, g)


def add_body(*refs, segs):
    n = len(segs)
    x_ref = refs[0]
    ps, rs = refs[1:1 + n], refs[1 + n:1 + 2 * n]
    g_ref, xo_ref, h_ref = refs[1 + 2 * n:]
    for p, r, seg in zip(ps, rs, segs):
        for src, dst, w in seg:
            a = (p[:, src:src + w].astype(F32) + r[:, src:src + w].astype(F32)).astype(BF16)
            xo_ref[:, dst:dst + w] = (x_ref[:, dst:dst + w].astype(F32) + a.astype(F32)).astype(BF16)
    h_ref[...] = norm_rows(xo_ref[...], g_ref[...])


def add_call(x, units, g):
    t, d = x.shape
    tb = 128
    row = pl.BlockSpec((tb, d), lambda r: (r, 0))
    ps, rs, segs = [u[0] for u in units], [u[1] for u in units], [u[2] for u in units]
    return pl.pallas_call(
        functools.partial(add_body, segs=segs),
        grid=(t // tb,),
        in_specs=[row] + [pl.BlockSpec((tb, a.shape[1]), lambda r: (r, 0)) for a in ps + rs]
        + [pl.BlockSpec((1, d), lambda r: (0, 0))],
        out_specs=[row, row],
        out_shape=[jax.ShapeDtypeStruct((t, d), BF16)] * 2,
        compiler_params=params(), cost_estimate=cost(12 * t * d, 10 * t * d),
    )(x, *ps, *rs, g)


def last_body(_, x_ref, p_ref, r_ref, *rest):
    o_ref = rest[-1]
    a = (p_ref[...].astype(F32) + r_ref[...].astype(F32)).astype(BF16)
    o_ref[...] = (x_ref[...].astype(F32) + a.astype(F32)).astype(BF16)


def last_call(x, unit, order, out_prev, row0, rows):
    p, r, seg = unit
    t, d = x.shape
    w = seg[0][2]
    per = d // 4 // w
    tb = 512
    dst = [s[1] // w for s in seg]
    step = (dst[1] - dst[0]) if len(dst) > 1 else 0
    assert all(dst[j] == dst[0] + j * step for j in range(len(dst)))
    base = dst[0]

    def x_map(j, i, o):
        return (i, base + j * step)

    def o_map(j, i, o):
        pb = base + j * step
        return (row0 // tb + i, o[pb // per] * per + pb % per)

    unit_spec = pl.BlockSpec((tb, w), lambda j, i, o: (i, j))
    args = [x, p, r] + ([out_prev] if out_prev is not None else [])
    return pl.pallas_call(
        last_body,
        grid_spec=pltpu.PrefetchScalarGridSpec(
            num_scalar_prefetch=1, grid=(len(seg), t // tb),
            in_specs=[pl.BlockSpec((tb, w), x_map), unit_spec, unit_spec] + [ANY] * (len(args) - 3),
            out_specs=pl.BlockSpec((tb, w), o_map)),
        out_shape=jax.ShapeDtypeStruct((rows, d), BF16),
        input_output_aliases={4: 0} if out_prev is not None else {},
        compiler_params=params(2), cost_estimate=cost(4 * t * w * len(seg), 8 * t * w * len(seg)),
    )(order, *args)


def solution(mesh):
    n_tp, n_fsdp = mesh.shape["tp"], mesh.shape["fsdp"]
    assert n_tp == 2 and n_fsdp == 4
    tok_spec = P(("dp", "fsdp"), None, None)
    gain_spec = P(None, "fsdp")
    col_spec = P(None, "fsdp", "tp")
    row_spec = P(None, "tp", "fsdp")
    cache_spec = P(None, ("dp", "fsdp"), None, "tp")
    far = [(i, i ^ 2) for i in range(4)]
    near = [(i, i ^ 1) for i in range(4)]
    swap = [(0, 1), (1, 0)]

    def device_fn(x_loc, g_attn, w_q, w_k, w_v, w_o, g_mlp, w_gate, w_up, w_down):
        _, seq, d = x_loc.shape
        n_layers = w_q.shape[0]
        qw, kw = w_q.shape[2], w_k.shape[2]
        f_loc = w_gate.shape[2]
        n_q, n_kv = qw // HEAD_DIM, kw // HEAD_DIM
        quarter = d // 4
        half_t = seq // 2
        assert sum(GU_BLOCKS) * GU_BN == f_loc
        dw = quarter // 2
        me = lax.axis_index("fsdp")
        order = jnp.stack([me, me ^ 1, me ^ 2, me ^ 3]).astype(jnp.int32)
        cos_t, sin_t = rope_tables(seq)
        x2 = x_loc.reshape(seq, d)

        def wide(l, i):
            lo, hi = sum(GU_BLOCKS[:i]) * GU_BN, sum(GU_BLOCKS[:i + 1]) * GU_BN
            return jnp.concatenate([w_gate[l][:, lo:hi], w_up[l][:, lo:hi]], axis=1)

        own = {O: w_o, GATE: w_gate, UP: w_up, DOWN: w_down, G: jnp.concatenate([g_attn, g_mlp], axis=0)}
        for l in range(n_layers):
            own[name_of(O, l)] = w_o[l]
            for i in range(len(GU_BLOCKS)):
                own[name_of(GU, l, i)] = wide(l, i)
            for i in range(2):
                own[name_of(D, l, i)] = w_down[l][:, i * dw:(i + 1) * dw]

        seg_a = [(0, 0, quarter), (quarter, quarter, quarter)]
        seg_own, seg_core = [(0, 0, quarter)], [(0, quarter, quarter)]
        seg_b = [(0, 2 * quarter, quarter), (quarter, 3 * quarter, quarter)]
        seg_d = [[(0, 2 * quarter + i * dw, dw), (dw, 3 * quarter + i * dw, dw)] for i in range(2)]

        xr, cr, nr, part, yr = {}, {}, {}, {}, {}
        hid, hn, qkv, ctx, acts = {}, {}, {}, {}, {}
        out, gains = [None], []

        def pieces(key):
            return [own[key], nr[key], xr[key], cr[key]]

        def kernel(name, dep, op, *idx):
            s, l = idx[-1], idx[-2] if op in (D, QKV, ATTN, OA, OB, ADDO, DA, DC, ADDM) else idx[0]
            if op == FIRST:
                if not gains:
                    rows = jnp.concatenate(pieces(G), axis=1).astype(F32)
                    gains.extend(rows[i:i + 1] for i in range(2 * n_layers))
                hid[s], hn[s] = first_call(dep(x2), order, gains[0], s * half_t, half_t)
                return hn[s]
            if op == QKV:
                rows = slice(s * half_t, (s + 1) * half_t)
                qkv[s] = qkv_call(dep(hn[s]), cos_t[rows], sin_t[rows], pieces(name_of(Q, l)), pieces(name_of(KV, l)),
                                  qw + kw)
                return qkv[s]
            if op == ATTN:
                ctx[s] = attn_call(dep(qkv[s]), [qkv[p] for p in range(s)], n_q, n_kv)
                return ctx[s]
            if op == OA:
                plan = [(0, l, 0), (0, l, dw), (1, l, 0), (1, l, dw)]
                part[name] = cols_call(dep(ctx[s]), [w_o, nr[O]], plan, dw)
                return part[name]
            if op in (DA, DC):
                w = w_down if op == DA else nr[DOWN]
                part[name] = cols_call(dep(acts[s]), [w], [(0, l, 0), (0, l, dw)], dw)
                return part[name]
            if op == OB:
                key = name_of(O, l)
                plan = [(0, None, 0), (0, None, dw), (1, None, 0), (1, None, dw)]
                part[name] = cols_call(dep(ctx[s]), [xr[key], cr[key]], plan, dw)
                return part[name]
            if op == D:
                key = name_of(D, l, idx[0])
                part[name] = cols_call(dep(acts[s]), [xr[key], cr[key]], [(0, None, 0), (1, None, 0)], dw)
                return part[name]
            if op == GU:
                i = idx[1]
                key = name_of(GU, l, i)
                acts[s] = gu_call(dep(hn[s]), w_gate, w_up, nr[GATE], nr[UP], xr[key], cr[key],
                                  acts[s] if i else None, sum(GU_BLOCKS[:i]), l, f_loc)
                return acts[s]
            if op == ADDO:
                tags = [name_of(w, l, s) for w in (OA, OB)]
                units = [(part[t], yr[t], g) for t, g in zip(tags, (seg_a, seg_b))]
                hid[s], hn[s] = add_call(dep(hid[s]), units, gains[n_layers + l])
                return hn[s]
            last_l = l if op == ADDM else n_layers - 1
            tags = [name_of(DA, last_l, s), name_of(DC, last_l, s), name_of(D, 0, last_l, s), name_of(D, 1, last_l, s)]
            segs = [seg_own, seg_core] + seg_d
            if op == ADDM:
                units = [(part[t], yr[t], g) for t, g in zip(tags, segs)]
                hid[s], hn[s] = add_call(dep(hid[s]), units, gains[l + 1])
                return hn[s]
            i = idx[0]
            unit = (part[tags[i]], yr[tags[i]], segs[i])
            out[0] = last_call(dep(hid[s]), unit, order, out[0], s * half_t, seq)
            return out[0]

        caches = []
        last = None
        for kind, *what in PLAN:
            name = name_of(*what)

            def dep(x):
                return x if last is None else lax.optimization_barrier((x, last))[0]

            if kind == X and what[0] == Q:
                own[name] = dep(w_q)[what[1]]
            elif kind == X and what[0] == KV:
                own[name] = jnp.concatenate([dep(w_k)[what[1]], dep(w_v)[what[1]]], axis=1)
            if kind == X:
                xr[name] = lax.ppermute(dep(own[name]), "fsdp", far)
            elif kind == C:
                cr[name] = lax.ppermute(dep(xr[name]), "fsdp", near)
            elif kind == N:
                nr[name] = lax.ppermute(own[name], "fsdp", near)
            elif kind == Y:
                yr[name] = lax.ppermute(part[name], "tp", swap)
            else:
                last = kernel(name, dep, *what)
            if kind == K and what[0] == QKV and what[-1] == 1:
                caches.append([jnp.concatenate([qkv[s][:, lo:lo + kw] for s in range(2)], axis=0)
                               for lo in (qw, qw + kw)])
        k_all, v_all = (jnp.stack([c[j] for c in caches])[:, None] for j in range(2))
        return out[0].reshape(1, seq, d), k_all, v_all

    return jax.shard_map(
        device_fn, mesh=mesh,
        in_specs=(tok_spec, gain_spec, col_spec, col_spec, col_spec, row_spec, gain_spec, col_spec, col_spec, row_spec),
        out_specs=(tok_spec, cache_spec, cache_spec), check_vma=False)
```

time: 4510 us -> 3210 us (0.71)
  Pallas kernels: 0 us -> 1490 us
  waiting for transfers between devices: 2730 us -> 1470 us
  matrix products: 1250 us -> 0 us
  other arithmetic: 285 us -> 58.2 us
  starting transfers between devices: 0.72 us -> 52.9 us
  local copies, waits for them, and re-layouts: 180 us -> 128 us
    pallas_call x0 -> x64, Pallas kernels: none -> 1490 us  [the longest x16 540 us: gu_call(): pl.pallas_call(functools.partial(gu_body, bn=bn, base=first * bn, tm=tm,...]
    ppermute x0 -> x71, waiting for transfers between devices: none -> 1470 us  [the longest x24 1100 us: device_fn(): yr[name] = lax.ppermute(part[name], 'tp', swap)]
    psum x4 -> x0, waiting for transfers between devices: 1380 us -> none  [the longest x2 703 us: local_layer(): mlp_out = lax.psum(mlp_part, 'tp')]
    all_gather x14 -> x0, waiting for transfers between devices: 1350 us -> none  [the longest x2 548 us: device_fn(): lax.all_gather(w_gate[layer_idx], 'fsdp', axis=0, tiled=True)]
    dot_general x30 -> x0, matrix products: 1250 us -> none  [the longest x2 254 us: local_layer(): jnp.einsum('bsm,mf->bsf', normed_mlp, w_up, preferred_element_type=jnp.fl...]
    reduce_sum x12 -> x0, other arithmetic: 199 us -> none  [the longest x8 133 us: causal_attention(): attn_probs = jax.nn.softmax(scores, axis=-1).astype(jnp.bfloat16)]
    squeeze x0 -> x9, local copies, waits for them, and re-layouts: none -> 59.4 us  [the longest x2 31.8 us: wide(): return jnp.concatenate([w_gate[l][:, lo:hi], w_up[l][:, lo:hi]], axis=1)]
    dot_general x4 -> x0, local copies, waits for them, and re-layouts: 55.7 us -> none  [the longest x2 42.6 us: local_layer(): jnp.einsum('bsm,mn->bsn', normed, w_q, preferred_element_type=jnp.float32)]
  transfers between devices with their start and end apart: 18 -> 71, of which waited for: 13 -> 36; matrix products, arithmetic and copies ran while one was open for 33% -> 5% of each run, Pallas kernels for 0% -> 46%
where the time goes in v1:
time: 3210 us; the launch traced here: 3200 us
  Pallas kernels  1490 us (46%)
  waiting for transfers between devices  1470 us (46%)
  local copies, waits for them, and re-layouts  128 us (4%)
  other arithmetic  58.2 us (2%)
  starting transfers between devices  52.9 us (2%)
    ppermute x24, waiting for transfers between devices, device_fn(): yr[name] = lax.ppermute(part[name], 'tp', swap)  1100 us
    pallas_call x16, Pallas kernels, gu_call(): pl.pallas_call(functools.partial(gu_body, bn=bn, base=first * bn, tm=tm,...  540 us
    pallas_call x24, Pallas kernels, cols_call(): pl.pallas_call(functools.partial(cols_body, plan=plan, n_w=len(ws), tm=tm...  422 us
    ppermute x19, waiting for transfers between devices, device_fn(): xr[name] = lax.ppermute(dep(own[name]), 'fsdp', far)  334 us
    pallas_call x4, Pallas kernels, attn_call(): pl.pallas_call(functools.partial(attn_body, n_past=len(past), bq=256, sca...  199 us
    pallas_call x4, Pallas kernels, qkv_call(): pl.pallas_call(functools.partial(qkv_body, bn=bn, n_rope=rope_cols // bn,...  155 us
    pallas_call x6, Pallas kernels, add_call(): pl.pallas_call(functools.partial(add_body, segs=segs), grid=(t // tb,), i...  105 us
  transfers between devices with their start and end apart: 71, of which 36 were waited for; matrix products, arithmetic and copies ran while one was open for 5% of the time, Pallas kernels for 46%

profile of v1, /device:TPU:0, one launch (start us, length us, event | category | flops | bytes accessed | tf_op | source)
XLA Modules:
  0.0 3196.7 jit_solution(337610881338934691)
XLA Ops:
  13.2 87.5 %collective-permute-done.1 = bf16[4,1024]{1,0:T(4,128)(2,1)S(1)} collective-permute-done((bf16[4,1024]{1,0:T(4,128)(2,1)S(1)}, bf16[4,1024]{1,0:T(4,128)(2,1)S(1)}, u32[]{:S(2)}, u32[]{:S(2)}) %collective-permute-start.1) | collective-permute-done | bytes 8224 | tf_op jit(solution)/shard_map/ppermute | solution.py:578
  170.4 38.9 %shard_map.123.q_ref.refs_0_.refs_1_.refs_2_ = bf16[1024,3072]{1,0:T(8,128)(2,1)} custom-call(bf16[1024,4096]{1,0:T(8,128)(2,1)} %get-tuple-element.121.a_hbm, f32[1024,128]{1,0:T(8,128)} %get-tuple-element.271.cos_ref, f32[1024,128]{1,0:T(8,128)} %get-tuple-element.261.sin_ref, bf16[1024,2048]{1,0:T(8,128)(2,1)} %slice_bitcast_fusion.9.refs_0_, ...), custom_call_target="tpu_custom_call" | custom-call | flops 25769803776 | bytes 39845888 | tf_op jit(solution)/shard_map/pallas_call | solution.py:174
  209.2 36.1 %shard_map.124.refs_0_ = bf16[1024,2048]{1,0:T(8,128)(2,1)} custom-call(bf16[1024,3072]{1,0:T(8,128)(2,1)} %shard_map.123.q_ref.refs_0_.refs_1_.refs_2_, bf16[1024,3072]{1,0:T(8,128)(2,1)} %shard_map.123.q_ref.refs_0_.refs_1_.refs_2_, bf16[1024,3072]{1,0:T(8,128)(2,1)} %shard_map.123.q_ref.refs_0_.refs_1_.refs_2_), custom_call_target="tpu_custom_call" | custom-call | flops 17179869184 | bytes 8388608 | tf_op jit(solution)/shard_map/pallas_call | solution.py:353
  318.5 38.8 %shard_map.127.q_ref.refs_1_.refs_3_ = bf16[1024,3072]{1,0:T(8,128)(2,1)} custom-call(bf16[1024,4096]{1,0:T(8,128)(2,1)} %get-tuple-element.128.a_hbm, f32[1024,128]{1,0:T(8,128)} %get-tuple-element.272.cos_ref, f32[1024,128]{1,0:T(8,128)} %get-tuple-element.260.sin_ref, bf16[1024,2048]{1,0:T(8,128)(2,1)} %slice_bitcast_fusion.9.refs_0_, ...), custom_call_target="tpu_custom_call" | custom-call | flops 25769803776 | bytes 39845888 | tf_op jit(solution)/shard_map/pallas_call | solution.py:174
  357.3 63.3 %shard_map.128.refs_0_ = bf16[1024,2048]{1,0:T(8,128)(2,1)} custom-call(bf16[1024,3072]{1,0:T(8,128)(2,1)} %shard_map.127.q_ref.refs_1_.refs_3_, bf16[1024,3072]{1,0:T(8,128)(2,1)} %shard_map.123.q_ref.refs_0_.refs_1_.refs_2_, bf16[1024,3072]{1,0:T(8,128)(2,1)} %shard_map.127.q_ref.refs_1_.refs_3_, ...), custom_call_target="tpu_custom_call" | custom-call | flops 51539607552 | bytes 8388608 | tf_op jit(solution)/shard_map/pallas_call | solution.py:353
  457.9 91.1 %collective-permute-done.13.refs_4_ = bf16[1024,2048]{1,0:T(8,128)(2,1)S(1)} collective-permute-done((bf16[1024,2048]{1,0:T(8,128)(2,1)S(1)}, bf16[1024,2048]{1,0:T(8,128)(2,1)S(1)}, u32[]{:S(2)}, u32[]{:S(2)}) %collective-permute-start.13) | collective-permute-done | bytes 4194336 | tf_op jit(solution)/shard_map/ppermute | solution.py:584
  568.6 38.8 %shard_map.132.refs_7_ = bf16[1024,6144]{1,0:T(8,128)(2,1)} custom-call(bf16[1024,4096]{1,0:T(8,128)(2,1)} %get-tuple-element.148.refs_0_, bf16[2,1024,6144]{2,1,0:T(8,128)(2,1)} %refs_1_.46, bf16[2,1024,6144]{2,1,0:T(8,128)(2,1)} %refs_2_.31, bf16[2,1024,6144]{2,1,0:T(8,128)(2,1)} %collective-permute-done.14.refs_3_, ...), custom_call_target="tpu_custom_call" | custom-call | flops 30064771072 | bytes 41418752 | tf_op jit(solution)/shard_map/pallas_call | solution.py:243
  646.3 38.5 %shard_map.133.refs_7_ = bf16[1024,6144]{1,0:T(8,128)(2,1)} custom-call(bf16[1024,4096]{1,0:T(8,128)(2,1)} %get-tuple-element.148.refs_0_, bf16[2,1024,6144]{2,1,0:T(8,128)(2,1)} %refs_1_.46, bf16[2,1024,6144]{2,1,0:T(8,128)(2,1)} %refs_2_.31, bf16[2,1024,6144]{2,1,0:T(8,128)(2,1)} %collective-permute-done.14.refs_3_, ...), custom_call_target="tpu_custom_call", output_to_operand_aliasing={{}: (7, {})} | custom-call | flops 30064771072 | bytes 41418752 | tf_op jit(solution)/shard_map/pallas_call | solution.py:243
  684.7 48.2 %collective-permute-done.21.refs_4_ = bf16[1024,2048]{1,0:T(8,128)(2,1)} collective-permute-done((bf16[1024,2048]{1,0:T(8,128)(2,1)}, bf16[1024,2048]{1,0:T(8,128)(2,1)}, u32[]{:S(2)}, u32[]{:S(2)}) %collective-permute-start.21) | collective-permute-done | bytes 4194336 | tf_op jit(solution)/shard_map/ppermute | solution.py:584
  732.9 88.6 %collective-permute-done.20.refs_3_ = bf16[1024,2048]{1,0:T(8,128)(2,1)} collective-permute-done((bf16[1024,2048]{1,0:T(8,128)(2,1)}, bf16[1024,2048]{1,0:T(8,128)(2,1)}, u32[]{:S(2)}, u32[]{:S(2)}) %collective-permute-start.20) | collective-permute-done | bytes 4194336 | tf_op jit(solution)/shard_map/ppermute | solution.py:584
  839.1 38.4 %shard_map.135.refs_7_ = bf16[1024,6144]{1,0:T(8,128)(2,1)} custom-call(bf16[1024,4096]{1,0:T(8,128)(2,1)} %get-tuple-element.153.refs_0_, bf16[2,1024,6144]{2,1,0:T(8,128)(2,1)} %refs_1_.46, bf16[2,1024,6144]{2,1,0:T(8,128)(2,1)} %refs_2_.31, bf16[2,1024,6144]{2,1,0:T(8,128)(2,1)} %collective-permute-done.14.refs_3_, ...), custom_call_target="tpu_custom_call" | custom-call | flops 30064771072 | bytes 41418752 | tf_op jit(solution)/shard_map/pallas_call | solution.py:243
  890.7 38.4 %shard_map.136.refs_7_ = bf16[1024,6144]{1,0:T(8,128)(2,1)} custom-call(bf16[1024,4096]{1,0:T(8,128)(2,1)} %get-tuple-element.153.refs_0_, bf16[2,1024,6144]{2,1,0:T(8,128)(2,1)} %refs_1_.46, bf16[2,1024,6144]{2,1,0:T(8,128)(2,1)} %refs_2_.31, bf16[2,1024,6144]{2,1,0:T(8,128)(2,1)} %collective-permute-done.14.refs_3_, ...), custom_call_target="tpu_custom_call", output_to_operand_aliasing={{}: (7, {})} | custom-call | flops 30064771072 | bytes 41418752 | tf_op jit(solution)/shard_map/pallas_call | solution.py:243
  929.1 33.7 %shard_map.137.refs_7_ = bf16[1024,6144]{1,0:T(8,128)(2,1)} custom-call(bf16[1024,4096]{1,0:T(8,128)(2,1)} %get-tuple-element.148.refs_0_, bf16[2,1024,6144]{2,1,0:T(8,128)(2,1)} %refs_1_.46, bf16[2,1024,6144]{2,1,0:T(8,128)(2,1)} %refs_2_.31, bf16[2,1024,6144]{2,1,0:T(8,128)(2,1)} %collective-permute-done.14.refs_3_, ...), custom_call_target="tpu_custom_call", output_to_operand_aliasing={{}: (7, {})} | custom-call | flops 25769803776 | bytes 36700160 | tf_op jit(solution)/shard_map/pallas_call | solution.py:243
  978.1 33.9 %shard_map.138.refs_7_ = bf16[1024,6144]{1,0:T(8,128)(2,1)} custom-call(bf16[1024,4096]{1,0:T(8,128)(2,1)} %get-tuple-element.153.refs_0_, bf16[2,1024,6144]{2,1,0:T(8,128)(2,1)} %refs_1_.46, bf16[2,1024,6144]{2,1,0:T(8,128)(2,1)} %refs_2_.31, bf16[2,1024,6144]{2,1,0:T(8,128)(2,1)} %collective-permute-done.14.refs_3_, ...), custom_call_target="tpu_custom_call", output_to_operand_aliasing={{}: (7, {})} | custom-call | flops 25769803776 | bytes 36700160 | tf_op jit(solution)/shard_map/pallas_call | solution.py:243
  1012.0 24.3 shard_map.139.refs_0_
  1074.9 24.3 shard_map.142.refs_0_
  1158.6 98.2 %collective-permute-done.29.refs_1_ = bf16[6144,512]{1,0:T(8,128)(2,1)} collective-permute-done((bf16[6144,512]{1,0:T(8,128)(2,1)}, bf16[6144,512]{1,0:T(8,128)(2,1)}, u32[]{:S(2)}, u32[]{:S(2)}) %collective-permute-start.29) | collective-permute-done | bytes 6291488 | tf_op jit(solution)/shard_map/ppermute | solution.py:578
  1326.4 25.1 collective-permute-done.31.refs_5_
  1352.6 43.8 %collective-permute-done.33.refs_7_ = bf16[1024,1024]{1,0:T(8,128)(2,1)} collective-permute-done((bf16[1024,1024]{1,0:T(8,128)(2,1)}, bf16[1024,1024]{1,0:T(8,128)(2,1)}, u32[]{:S(2)}, u32[]{:S(2)}) %collective-permute-start.33) | collective-permute-done | bytes 2097184 | tf_op jit(solution)/shard_map/ppermute | solution.py:584
  1396.5 44.2 %collective-permute-done.34.refs_8_ = bf16[1024,1024]{1,0:T(8,128)(2,1)} collective-permute-done((bf16[1024,1024]{1,0:T(8,128)(2,1)}, bf16[1024,1024]{1,0:T(8,128)(2,1)}, u32[]{:S(2)}, u32[]{:S(2)}) %collective-permute-start.34) | collective-permute-done | bytes 2097184 | tf_op jit(solution)/shard_map/ppermute | solution.py:584
  1471.4 38.8 %shard_map.150.q_ref.refs_0_.refs_1_.refs_2_ = bf16[1024,3072]{1,0:T(8,128)(2,1)} custom-call(bf16[1024,4096]{1,0:T(8,128)(2,1)} %get-tuple-element.166.a_hbm, f32[1024,128]{1,0:T(8,128)} %get-tuple-element.271.cos_ref, f32[1024,128]{1,0:T(8,128)} %get-tuple-element.261.sin_ref, bf16[1024,2048]{1,0:T(8,128)(2,1)} %slice_bitcast_fusion.7.refs_0_, ...), custom_call_target="tpu_custom_call" | custom-call | flops 25769803776 | bytes 39845888 | tf_op jit(solution)/shard_map/pallas_call | solution.py:174
  1510.2 36.2 %shard_map.151.refs_0_ = bf16[1024,2048]{1,0:T(8,128)(2,1)} custom-call(bf16[1024,3072]{1,0:T(8,128)(2,1)} %shard_map.150.q_ref.refs_0_.refs_1_.refs_2_, bf16[1024,3072]{1,0:T(8,128)(2,1)} %shard_map.150.q_ref.refs_0_.refs_1_.refs_2_, bf16[1024,3072]{1,0:T(8,128)(2,1)} %shard_map.150.q_ref.refs_0_.refs_1_.refs_2_), custom_call_target="tpu_custom_call" | custom-call | flops 17179869184 | bytes 8388608 | tf_op jit(solution)/shard_map/pallas_call | solution.py:353
  1571.5 38.2 %collective-permute-done.42.refs_6_ = bf16[1024,1024]{1,0:T(8,128)(2,1)} collective-permute-done((bf16[1024,1024]{1,0:T(8,128)(2,1)}, bf16[1024,1024]{1,0:T(8,128)(2,1)}, u32[]{:S(2)}, u32[]{:S(2)}) %collective-permute-start.42) | collective-permute-done | bytes 2097184 | tf_op jit(solution)/shard_map/ppermute | solution.py:584
  1610.8 43.8 %collective-permute-done.41.refs_5_ = bf16[1024,1024]{1,0:T(8,128)(2,1)} collective-permute-done((bf16[1024,1024]{1,0:T(8,128)(2,1)}, bf16[1024,1024]{1,0:T(8,128)(2,1)}, u32[]{:S(2)}, u32[]{:S(2)}) %collective-permute-start.41) | collective-permute-done | bytes 2097184 | tf_op jit(solution)/shard_map/ppermute | solution.py:584
  1654.7 44.9 %collective-permute-done.44.refs_8_ = bf16[1024,1024]{1,0:T(8,128)(2,1)} collective-permute-done((bf16[1024,1024]{1,0:T(8,128)(2,1)}, bf16[1024,1024]{1,0:T(8,128)(2,1)}, u32[]{:S(2)}, u32[]{:S(2)}) %collective-permute-start.44) | collective-permute-done | bytes 2097184 | tf_op jit(solution)/shard_map/ppermute | solution.py:584
  1699.6 44.3 %collective-permute-done.43.refs_7_ = bf16[1024,1024]{1,0:T(8,128)(2,1)} collective-permute-done((bf16[1024,1024]{1,0:T(8,128)(2,1)}, bf16[1024,1024]{1,0:T(8,128)(2,1)}, u32[]{:S(2)}, u32[]{:S(2)}) %collective-permute-start.43) | collective-permute-done | bytes 2097184 | tf_op jit(solution)/shard_map/ppermute | solution.py:584
  1775.2 38.9 %shard_map.155.q_ref.refs_1_.refs_3_ = bf16[1024,3072]{1,0:T(8,128)(2,1)} custom-call(bf16[1024,4096]{1,0:T(8,128)(2,1)} %get-tuple-element.183.a_hbm, f32[1024,128]{1,0:T(8,128)} %get-tuple-element.272.cos_ref, f32[1024,128]{1,0:T(8,128)} %get-tuple-element.260.sin_ref, bf16[1024,2048]{1,0:T(8,128)(2,1)} %slice_bitcast_fusion.7.refs_0_, ...), custom_call_target="tpu_custom_call" | custom-call | flops 25769803776 | bytes 39845888 | tf_op jit(solution)/shard_map/pallas_call | solution.py:174
  1814.1 63.3 %shard_map.156.refs_0_ = bf16[1024,2048]{1,0:T(8,128)(2,1)} custom-call(bf16[1024,3072]{1,0:T(8,128)(2,1)} %shard_map.155.q_ref.refs_1_.refs_3_, bf16[1024,3072]{1,0:T(8,128)(2,1)} %shard_map.150.q_ref.refs_0_.refs_1_.refs_2_, bf16[1024,3072]{1,0:T(8,128)(2,1)} %shard_map.155.q_ref.refs_1_.refs_3_, ...), custom_call_target="tpu_custom_call" | custom-call | flops 51539607552 | bytes 8388608 | tf_op jit(solution)/shard_map/pallas_call | solution.py:353
  1915.3 91.4 %collective-permute-done.47.refs_3_ = bf16[1024,2048]{1,0:T(8,128)(2,1)S(1)} collective-permute-done((bf16[1024,2048]{1,0:T(8,128)(2,1)S(1)}, bf16[1024,2048]{1,0:T(8,128)(2,1)S(1)}, u32[]{:S(2)}, u32[]{:S(2)}) %collective-permute-start.47) | collective-permute-done | bytes 4194336 | tf_op jit(solution)/shard_map/ppermute | solution.py:584
  2008.8 87.1 %collective-permute-done.48.refs_4_ = bf16[1024,2048]{1,0:T(8,128)(2,1)S(1)} collective-permute-done((bf16[1024,2048]{1,0:T(8,128)(2,1)}, bf16[1024,2048]{1,0:T(8,128)(2,1)S(1)}, u32[]{:S(2)}, u32[]{:S(2)}) %collective-permute-start.48) | collective-permute-done | bytes 4194336 | tf_op jit(solution)/shard_map/ppermute | solution.py:584
  2115.5 38.7 %shard_map.160.refs_7_ = bf16[1024,6144]{1,0:T(8,128)(2,1)} custom-call(bf16[1024,4096]{1,0:T(8,128)(2,1)} %get-tuple-element.205.refs_0_, bf16[2,1024,6144]{2,1,0:T(8,128)(2,1)} %refs_1_.46, bf16[2,1024,6144]{2,1,0:T(8,128)(2,1)} %refs_2_.31, bf16[2,1024,6144]{2,1,0:T(8,128)(2,1)} %collective-permute-done.14.refs_3_, ...), custom_call_target="tpu_custom_call" | custom-call | flops 30064771072 | bytes 41418752 | tf_op jit(solution)/shard_map/pallas_call | solution.py:243
  2176.6 38.4 %shard_map.161.refs_7_ = bf16[1024,6144]{1,0:T(8,128)(2,1)} custom-call(bf16[1024,4096]{1,0:T(8,128)(2,1)} %get-tuple-element.205.refs_0_, bf16[2,1024,6144]{2,1,0:T(8,128)(2,1)} %refs_1_.46, bf16[2,1024,6144]{2,1,0:T(8,128)(2,1)} %refs_2_.31, bf16[2,1024,6144]{2,1,0:T(8,128)(2,1)} %collective-permute-done.14.refs_3_, ...), custom_call_target="tpu_custom_call", output_to_operand_aliasing={{}: (7, {})} | custom-call | flops 30064771072 | bytes 41418752 | tf_op jit(solution)/shard_map/pallas_call | solution.py:243
  2215.0 47.4 %collective-permute-done.54.refs_4_ = bf16[1024,2048]{1,0:T(8,128)(2,1)} collective-permute-done((bf16[1024,2048]{1,0:T(8,128)(2,1)}, bf16[1024,2048]{1,0:T(8,128)(2,1)}, u32[]{:S(2)}, u32[]{:S(2)}) %collective-permute-start.54) | collective-permute-done | bytes 4194336 | tf_op jit(solution)/shard_map/ppermute | solution.py:584
  2262.4 89.4 %collective-permute-done.53.refs_3_ = bf16[1024,2048]{1,0:T(8,128)(2,1)} collective-permute-done((bf16[1024,2048]{1,0:T(8,128)(2,1)}, bf16[1024,2048]{1,0:T(8,128)(2,1)}, u32[]{:S(2)}, u32[]{:S(2)}) %collective-permute-start.53) | collective-permute-done | bytes 4194336 | tf_op jit(solution)/shard_map/ppermute | solution.py:584
  2369.4 38.3 %shard_map.163.refs_7_ = bf16[1024,6144]{1,0:T(8,128)(2,1)} custom-call(bf16[1024,4096]{1,0:T(8,128)(2,1)} %get-tuple-element.210.refs_0_, bf16[2,1024,6144]{2,1,0:T(8,128)(2,1)} %refs_1_.46, bf16[2,1024,6144]{2,1,0:T(8,128)(2,1)} %refs_2_.31, bf16[2,1024,6144]{2,1,0:T(8,128)(2,1)} %collective-permute-done.14.refs_3_, ...), custom_call_target="tpu_custom_call" | custom-call | flops 30064771072 | bytes 41418752 | tf_op jit(solution)/shard_map/pallas_call | solution.py:243
  2407.7 38.4 %shard_map.164.refs_7_ = bf16[1024,6144]{1,0:T(8,128)(2,1)} custom-call(bf16[1024,4096]{1,0:T(8,128)(2,1)} %get-tuple-element.210.refs_0_, bf16[2,1024,6144]{2,1,0:T(8,128)(2,1)} %refs_1_.46, bf16[2,1024,6144]{2,1,0:T(8,128)(2,1)} %refs_2_.31, bf16[2,1024,6144]{2,1,0:T(8,128)(2,1)} %collective-permute-done.14.refs_3_, ...), custom_call_target="tpu_custom_call", output_to_operand_aliasing={{}: (7, {})} | custom-call | flops 30064771072 | bytes 41418752 | tf_op jit(solution)/shard_map/pallas_call | solution.py:243
  2456.6 33.7 %shard_map.165.refs_7_ = bf16[1024,6144]{1,0:T(8,128)(2,1)} custom-call(bf16[1024,4096]{1,0:T(8,128)(2,1)} %get-tuple-element.205.refs_0_, bf16[2,1024,6144]{2,1,0:T(8,128)(2,1)} %refs_1_.46, bf16[2,1024,6144]{2,1,0:T(8,128)(2,1)} %refs_2_.31, bf16[2,1024,6144]{2,1,0:T(8,128)(2,1)} %collective-permute-done.14.refs_3_, ...), custom_call_target="tpu_custom_call", output_to_operand_aliasing={{}: (7, {})} | custom-call | flops 25769803776 | bytes 36700160 | tf_op jit(solution)/shard_map/pallas_call | solution.py:243
  2490.3 33.9 %shard_map.166.refs_7_ = bf16[1024,6144]{1,0:T(8,128)(2,1)} custom-call(bf16[1024,4096]{1,0:T(8,128)(2,1)} %get-tuple-element.210.refs_0_, bf16[2,1024,6144]{2,1,0:T(8,128)(2,1)} %refs_1_.46, bf16[2,1024,6144]{2,1,0:T(8,128)(2,1)} %refs_2_.31, bf16[2,1024,6144]{2,1,0:T(8,128)(2,1)} %collective-permute-done.14.refs_3_, ...), custom_call_target="tpu_custom_call", output_to_operand_aliasing={{}: (7, {})} | custom-call | flops 25769803776 | bytes 36700160 | tf_op jit(solution)/shard_map/pallas_call | solution.py:243
  2524.2 21.2 collective-permute-done.57.refs_5_
  2552.9 24.2 shard_map.167.refs_0_
  2616.0 24.2 shard_map.170.refs_0_
  2733.0 88.9 %collective-permute-done.61.refs_1_ = bf16[6144,512]{1,0:T(8,128)(2,1)} collective-permute-done((bf16[6144,512]{1,0:T(8,128)(2,1)}, bf16[6144,512]{1,0:T(8,128)(2,1)}, u32[]{:S(2)}, u32[]{:S(2)}) %collective-permute-start.61) | collective-permute-done | bytes 6291488 | tf_op jit(solution)/shard_map/ppermute | solution.py:578
  2872.0 49.5 %collective-permute-done.64.r_ref = bf16[1024,1024]{1,0:T(8,128)(2,1)} collective-permute-done((bf16[1024,1024]{1,0:T(8,128)(2,1)}, bf16[1024,1024]{1,0:T(8,128)(2,1)}, u32[]{:S(2)}, u32[]{:S(2)}) %collective-permute-start.64) | collective-permute-done | bytes 2097184 | tf_op jit(solution)/shard_map/ppermute | solution.py:584
  2922.4 44.0 %collective-permute-done.65.r_ref = bf16[1024,1024]{1,0:T(8,128)(2,1)} collective-permute-done((bf16[1024,1024]{1,0:T(8,128)(2,1)}, bf16[1024,1024]{1,0:T(8,128)(2,1)}, u32[]{:S(2)}, u32[]{:S(2)}) %collective-permute-start.65) | collective-permute-done | bytes 2097184 | tf_op jit(solution)/shard_map/ppermute | solution.py:584
  2967.3 44.0 %collective-permute-done.63.r_ref = bf16[1024,1024]{1,0:T(8,128)(2,1)} collective-permute-done((bf16[1024,1024]{1,0:T(8,128)(2,1)}, bf16[1024,1024]{1,0:T(8,128)(2,1)}, u32[]{:S(2)}, u32[]{:S(2)}) %collective-permute-start.63) | collective-permute-done | bytes 2097184 | tf_op jit(solution)/shard_map/ppermute | solution.py:584
  3043.2 58.1 %collective-permute-done.67.r_ref = bf16[1024,1024]{1,0:T(8,128)(2,1)} collective-permute-done((bf16[1024,1024]{1,0:T(8,128)(2,1)}, bf16[1024,1024]{1,0:T(8,128)(2,1)}, u32[]{:S(2)}, u32[]{:S(2)}) %collective-permute-start.67) | collective-permute-done | bytes 2097184 | tf_op jit(solution)/shard_map/ppermute | solution.py:584
  3112.5 33.7 %collective-permute-done.69.r_ref = bf16[1024,1024]{1,0:T(8,128)(2,1)} collective-permute-done((bf16[1024,1024]{1,0:T(8,128)(2,1)}, bf16[1024,1024]{1,0:T(8,128)(2,1)}, u32[]{:S(2)}, u32[]{:S(2)}) %collective-permute-start.69) | collective-permute-done | bytes 2097184 | tf_op jit(solution)/shard_map/ppermute | solution.py:584
  3151.8 38.8 %collective-permute-done.70.r_ref = bf16[1024,1024]{1,0:T(8,128)(2,1)} collective-permute-done((bf16[1024,1024]{1,0:T(8,128)(2,1)}, bf16[1024,1024]{1,0:T(8,128)(2,1)}, u32[]{:S(2)}, u32[]{:S(2)}) %collective-permute-start.70) | collective-permute-done | bytes 2097184 | tf_op jit(solution)/shard_map/ppermute | solution.py:584
  (244 shorter events, 909.3 us)
Async XLA Ops:
  5.6 120.9 %collective-permute-start.4 = (bf16[1024,2048]{1,0:T(8,128)(2,1)}, bf16[1024,2048]{1,0:T(8,128)(2,1)}, u32[]{:S(2)}, u32[]{:S(2)}) collective-permute-start(bf16[1024,2048]{1,0:T(8,128)(2,1)} %slice_bitcast_fusion.9.refs_0_), channel_id=1, source_target_pairs={{0,2},{1,3},{2,0},{3,1},{4,6},{5,7},{6,4},{7,5}} | collective-permute-start | bytes 12582920 | tf_op jit(solution)/shard_map/ppermute | solution.py:578
  9.0 92.3 %collective-permute-start = (bf16[4,1024]{1,0:T(4,128)(2,1)S(1)}, bf16[4,1024]{1,0:T(4,128)(2,1)S(1)}, u32[]{:S(2)}, u32[]{:S(2)}) collective-permute-start(bf16[4,1024]{1,0:T(4,128)(2,1)S(1)} %pad_maximum_fusion.12), channel_id=1, source_target_pairs={{0,1},{1,0},{2,3},{3,2},{4,5},{5,4},{6,7},{7,6}} | collective-permute-start | bytes 24584 | tf_op jit(solution)/shard_map/ppermute | solution.py:582
  9.0 160.8 %collective-permute-start.3 = (bf16[1024,2048]{1,0:T(8,128)(2,1)}, bf16[1024,2048]{1,0:T(8,128)(2,1)}, u32[]{:S(2)}, u32[]{:S(2)}) collective-permute-start(bf16[1024,2048]{1,0:T(8,128)(2,1)} %slice_bitcast_fusion.9.refs_0_), channel_id=1, source_target_pairs={{0,1},{1,0},{2,3},{3,2},{4,5},{5,4},{6,7},{7,6}} | collective-permute-start | bytes 12582920 | tf_op jit(solution)/shard_map/ppermute | solution.py:582
  11.2 134.5 %collective-permute-start.7 = (bf16[1024,1024]{1,0:T(8,128)(2,1)}, bf16[1024,1024]{1,0:T(8,128)(2,1)}, u32[]{:S(2)}, u32[]{:S(2)}) collective-permute-start(bf16[1024,1024]{1,0:T(8,128)(2,1)} %pad_maximum_fusion.8.refs_4_), channel_id=1, source_target_pairs={{0,2},{1,3},{2,0},{3,1},{4,6},{5,7},{6,4},{7,5}} | collective-permute-start | bytes 6291464 | tf_op jit(solution)/shard_map/ppermute | solution.py:578
  133.0 112.3 %collective-permute-start.10 = (bf16[2048,1024]{1,0:T(8,128)(2,1)}, bf16[2048,1024]{1,0:T(8,128)(2,1)}, u32[]{:S(2)}, u32[]{:S(2)}) collective-permute-start(bf16[2048,1024]{1,0:T(8,128)(2,1)} %get-tuple-element.251), channel_id=1, source_target_pairs={{0,2},{1,3},{2,0},{3,1},{4,6},{5,7},{6,4},{7,5}} | collective-permute-start | bytes 12582920 | tf_op jit(solution)/shard_map/ppermute | solution.py:578
  169.4 119.7 %collective-permute-start.9 = (bf16[2,2048,1024]{2,1,0:T(8,128)(2,1)}, bf16[2,2048,1024]{2,1,0:T(8,128)(2,1)}, u32[]{:S(2)}, u32[]{:S(2)}) collective-permute-start(bf16[2,2048,1024]{2,1,0:T(8,128)(2,1)} %refs_1_.37), channel_id=1, source_target_pairs={{0,1},{1,0},{2,3},{3,2},{4,5},{5,4},{6,7},{7,6}} | collective-permute-start | bytes 25165832 | tf_op jit(solution)/shard_map/ppermute | solution.py:582
  169.9 398.7 %collective-permute-start.14 = (bf16[2,1024,6144]{2,1,0:T(8,128)(2,1)}, bf16[2,1024,6144]{2,1,0:T(8,128)(2,1)}, u32[]{:S(2)}, u32[]{:S(2)}) collective-permute-start(bf16[2,1024,6144]{2,1,0:T(8,128)(2,1)} %refs_1_.46), channel_id=1, source_target_pairs={{0,1},{1,0},{2,3},{3,2},{4,5},{5,4},{6,7},{7,6}} | collective-permute-start | bytes 75497480 | tf_op jit(solution)/shard_map/ppermute | solution.py:582
  169.9 398.7 %collective-permute-start.15 = (bf16[2,1024,6144]{2,1,0:T(8,128)(2,1)}, bf16[2,1024,6144]{2,1,0:T(8,128)(2,1)}, u32[]{:S(2)}, u32[]{:S(2)}) collective-permute-start(bf16[2,1024,6144]{2,1,0:T(8,128)(2,1)} %refs_2_.31), channel_id=1, source_target_pairs={{0,1},{1,0},{2,3},{3,2},{4,5},{5,4},{6,7},{7,6}} | collective-permute-start | bytes 75497480 | tf_op jit(solution)/shard_map/ppermute | solution.py:582
  287.0 161.6 %collective-permute-start.16 = (bf16[1024,3584]{1,0:T(8,128)(2,1)}, bf16[1024,3584]{1,0:T(8,128)(2,1)}, u32[]{:S(2)}, u32[]{:S(2)}) collective-permute-start(bf16[1024,3584]{1,0:T(8,128)(2,1)} %pad_maximum_fusion), channel_id=1, source_target_pairs={{0,2},{1,3},{2,0},{3,1},{4,6},{5,7},{6,4},{7,5}} | collective-permute-start | bytes 22020104 | tf_op jit(solution)/shard_map/ppermute | solution.py:578
  303.0 153.3 %collective-permute-start.12 = (bf16[1024,2048]{1,0:T(8,128)(2,1)}, bf16[1024,2048]{1,0:T(8,128)(2,1)}, u32[]{:S(2)}, u32[]{:S(2)}) collective-permute-start(bf16[1024,2048]{1,0:T(8,128)(2,1)} %shard_map.125.refs_1_), channel_id=1, source_target_pairs={{0,4},{4,0},{1,5},{5,1},{2,6},{6,2},{3,7},{7,3}} | collective-permute-start | bytes 12582920 | tf_op jit(solution)/shard_map/ppermute | solution.py:584
  448.6 120.0 %collective-permute-start.17 = (bf16[1024,3584]{1,0:T(8,128)(2,1)}, bf16[1024,3584]{1,0:T(8,128)(2,1)}, u32[]{:S(2)}, u32[]{:S(2)}) collective-permute-start(bf16[1024,3584]{1,0:T(8,128)(2,1)} %collective-permute-done.16.refs_5_), channel_id=1, source_target_pairs={{0,1},{1,0},{2,3},{3,2},{4,5},{5,4},{6,7},{7,6}} | collective-permute-start | bytes 22020104 | tf_op jit(solution)/shard_map/ppermute | solution.py:580
  455.4 160.7 %collective-permute-start.18 = (bf16[1024,3584]{1,0:T(8,128)(2,1)}, bf16[1024,3584]{1,0:T(8,128)(2,1)}, u32[]{:S(2)}, u32[]{:S(2)}) collective-permute-start(bf16[1024,3584]{1,0:T(8,128)(2,1)} %pad_maximum_fusion.1), channel_id=1, source_target_pairs={{0,2},{1,3},{2,0},{3,1},{4,6},{5,7},{6,4},{7,5}} | collective-permute-start | bytes 22020104 | tf_op jit(solution)/shard_map/ppermute | solution.py:578
  456.3 92.7 %collective-permute-start.13 = (bf16[1024,2048]{1,0:T(8,128)(2,1)S(1)}, bf16[1024,2048]{1,0:T(8,128)(2,1)S(1)}, u32[]{:S(2)}, u32[]{:S(2)}) collective-permute-start(bf16[1024,2048]{1,0:T(8,128)(2,1)S(1)} %copy-done.3), channel_id=1, source_target_pairs={{0,4},{4,0},{1,5},{5,1},{2,6},{6,2},{3,7},{7,3}} | collective-permute-start | bytes 12582920 | tf_op jit(solution)/shard_map/ppermute | solution.py:584
  616.1 439.5 %collective-permute-start.26 = (bf16[2,6144,1024]{2,1,0:T(8,128)(2,1)}, bf16[2,6144,1024]{2,1,0:T(8,128)(2,1)}, u32[]{:S(2)}, u32[]{:S(2)}) collective-permute-start(bf16[2,6144,1024]{2,1,0:T(8,128)(2,1)} %refs_1_.47), channel_id=1, source_target_pairs={{0,1},{1,0},{2,3},{3,2},{4,5},{5,4},{6,7},{7,6}} | collective-permute-start | bytes 75497480 | tf_op jit(solution)/shard_map/ppermute | solution.py:582
  638.3 239.3 %collective-permute-start.22 = (bf16[1024,3072]{1,0:T(8,128)(2,1)}, bf16[1024,3072]{1,0:T(8,128)(2,1)}, u32[]{:S(2)}, u32[]{:S(2)}) collective-permute-start(bf16[1024,3072]{1,0:T(8,128)(2,1)} %pad_maximum_fusion.4), channel_id=1, source_target_pairs={{0,2},{1,3},{2,0},{3,1},{4,6},{5,7},{6,4},{7,5}} | collective-permute-start | bytes 18874376 | tf_op jit(solution)/shard_map/ppermute | solution.py:578
  639.2 93.8 %collective-permute-start.21 = (bf16[1024,2048]{1,0:T(8,128)(2,1)}, bf16[1024,2048]{1,0:T(8,128)(2,1)}, u32[]{:S(2)}, u32[]{:S(2)}) collective-permute-start(bf16[1024,2048]{1,0:T(8,128)(2,1)} %shard_map.130.refs_2_), channel_id=1, source_target_pairs={{0,4},{4,0},{1,5},{5,1},{2,6},{6,2},{3,7},{7,3}} | collective-permute-start | bytes 12582920 | tf_op jit(solution)/shard_map/ppermute | solution.py:584
  640.8 180.7 %collective-permute-start.20 = (bf16[1024,2048]{1,0:T(8,128)(2,1)}, bf16[1024,2048]{1,0:T(8,128)(2,1)}, u32[]{:S(2)}, u32[]{:S(2)}) collective-permute-start(bf16[1024,2048]{1,0:T(8,128)(2,1)} %shard_map.129.refs_1_), channel_id=1, source_target_pairs={{0,4},{4,0},{1,5},{5,1},{2,6},{6,2},{3,7},{7,3}} | collective-permute-start | bytes 12582920 | tf_op jit(solution)/shard_map/ppermute | solution.py:584
  883.7 93.3 %collective-permute-start.24 = (bf16[1024,2048]{1,0:T(8,128)(2,1)}, bf16[1024,2048]{1,0:T(8,128)(2,1)}, u32[]{:S(2)}, u32[]{:S(2)}) collective-permute-start(bf16[1024,2048]{1,0:T(8,128)(2,1)} %pad_maximum_fusion.6), channel_id=1, source_target_pairs={{0,2},{1,3},{2,0},{3,1},{4,6},{5,7},{6,4},{7,5}} | collective-permute-start | bytes 12582920 | tf_op jit(solution)/shard_map/ppermute | solution.py:578
  977.0 141.6 %collective-permute-start.27 = (bf16[6144,512]{1,0:T(8,128)(2,1)}, bf16[6144,512]{1,0:T(8,128)(2,1)}, u32[]{:S(2)}, u32[]{:S(2)}) collective-permute-start(bf16[6144,512]{1,0:T(8,128)(2,1)} %get-tuple-element.157), channel_id=1, source_target_pairs={{0,2},{1,3},{2,0},{3,1},{4,6},{5,7},{6,4},{7,5}} | collective-permute-start | bytes 18874376 | tf_op jit(solution)/shard_map/ppermute | solution.py:578
  1118.8 138.0 %collective-permute-start.29 = (bf16[6144,512]{1,0:T(8,128)(2,1)}, bf16[6144,512]{1,0:T(8,128)(2,1)}, u32[]{:S(2)}, u32[]{:S(2)}) collective-permute-start(bf16[6144,512]{1,0:T(8,128)(2,1)} %get-tuple-element.160), channel_id=1, source_target_pairs={{0,2},{1,3},{2,0},{3,1},{4,6},{5,7},{6,4},{7,5}} | collective-permute-start | bytes 18874376 | tf_op jit(solution)/shard_map/ppermute | solution.py:578
  1256.9 201.0 %collective-permute-start.36 = (bf16[1024,2048]{1,0:T(8,128)(2,1)}, bf16[1024,2048]{1,0:T(8,128)(2,1)}, u32[]{:S(2)}, u32[]{:S(2)}) collective-permute-start(bf16[1024,2048]{1,0:T(8,128)(2,1)} %slice_bitcast_fusion.7.refs_0_), channel_id=1, source_target_pairs={{0,2},{1,3},{2,0},{3,1},{4,6},{5,7},{6,4},{7,5}} | collective-permute-start | bytes 12582920 | tf_op jit(solution)/shard_map/ppermute | solution.py:578
  1259.8 136.7 %collective-permute-start.33 = (bf16[1024,1024]{1,0:T(8,128)(2,1)}, bf16[1024,1024]{1,0:T(8,128)(2,1)}, u32[]{:S(2)}, u32[]{:S(2)}) collective-permute-start(bf16[1024,1024]{1,0:T(8,128)(2,1)} %shard_map.145.refs_3_), channel_id=1, source_target_pairs={{0,4},{4,0},{1,5},{5,1},{2,6},{6,2},{3,7},{7,3}} | collective-permute-start | bytes 6291464 | tf_op jit(solution)/shard_map/ppermute | solution.py:584
  1286.7 154.0 %collective-permute-start.34 = (bf16[1024,1024]{1,0:T(8,128)(2,1)}, bf16[1024,1024]{1,0:T(8,128)(2,1)}, u32[]{:S(2)}, u32[]{:S(2)}) collective-permute-start(bf16[1024,1024]{1,0:T(8,128)(2,1)} %shard_map.146.refs_4_), channel_id=1, source_target_pairs={{0,4},{4,0},{1,5},{5,1},{2,6},{6,2},{3,7},{7,3}} | collective-permute-start | bytes 6291464 | tf_op jit(solution)/shard_map/ppermute | solution.py:584
  1326.3 142.1 %collective-permute-start.35 = (bf16[1024,2048]{1,0:T(8,128)(2,1)}, bf16[1024,2048]{1,0:T(8,128)(2,1)}, u32[]{:S(2)}, u32[]{:S(2)}) collective-permute-start(bf16[1024,2048]{1,0:T(8,128)(2,1)} %slice_bitcast_fusion.7.refs_0_), channel_id=1, source_target_pairs={{0,1},{1,0},{2,3},{3,2},{4,5},{5,4},{6,7},{7,6}} | collective-permute-start | bytes 12582920 | tf_op jit(solution)/shard_map/ppermute | solution.py:582
  1351.5 106.9 %collective-permute-start.39 = (bf16[1024,1024]{1,0:T(8,128)(2,1)}, bf16[1024,1024]{1,0:T(8,128)(2,1)}, u32[]{:S(2)}, u32[]{:S(2)}) collective-permute-start(bf16[1024,1024]{1,0:T(8,128)(2,1)} %pad_maximum_fusion.9.refs_4_), channel_id=1, source_target_pairs={{0,2},{1,3},{2,0},{3,1},{4,6},{5,7},{6,4},{7,5}} | collective-permute-start | bytes 6291464 | tf_op jit(solution)/shard_map/ppermute | solution.py:578
  1458.5 102.3 %collective-permute-start.45 = (bf16[2048,1024]{1,0:T(8,128)(2,1)}, bf16[2048,1024]{1,0:T(8,128)(2,1)}, u32[]{:S(2)}, u32[]{:S(2)}) collective-permute-start(bf16[2048,1024]{1,0:T(8,128)(2,1)} %get-tuple-element.181), channel_id=1, source_target_pairs={{0,2},{1,3},{2,0},{3,1},{4,6},{5,7},{6,4},{7,5}} | collective-permute-start | bytes 12582920 | tf_op jit(solution)/shard_map/ppermute | solution.py:578
  1560.7 200.5 %collective-permute-start.46 = (bf16[2048,1024]{1,0:T(8,128)(2,1)}, bf16[2048,1024]{1,0:T(8,128)(2,1)}, u32[]{:S(2)}, u32[]{:S(2)}) collective-permute-start(bf16[2048,1024]{1,0:T(8,128)(2,1)} %collective-permute-done.45.refs_1_), channel_id=1, source_target_pairs={{0,1},{1,0},{2,3},{3,2},{4,5},{5,4},{6,7},{7,6}} | collective-permute-start | bytes 12582920 | tf_op jit(solution)/shard_map/ppermute | solution.py:580
  1562.9 136.7 %collective-permute-start.44 = (bf16[1024,1024]{1,0:T(8,128)(2,1)}, bf16[1024,1024]{1,0:T(8,128)(2,1)}, u32[]{:S(2)}, u32[]{:S(2)}) collective-permute-start(bf16[1024,1024]{1,0:T(8,128)(2,1)} %shard_map.148.refs_4_), channel_id=1, source_target_pairs={{0,4},{4,0},{1,5},{5,1},{2,6},{6,2},{3,7},{7,3}} | collective-permute-start | bytes 6291464 | tf_op jit(solution)/shard_map/ppermute | solution.py:584
  1564.6 179.4 %collective-permute-start.43 = (bf16[1024,1024]{1,0:T(8,128)(2,1)}, bf16[1024,1024]{1,0:T(8,128)(2,1)}, u32[]{:S(2)}, u32[]{:S(2)}) collective-permute-start(bf16[1024,1024]{1,0:T(8,128)(2,1)} %shard_map.147.refs_3_), channel_id=1, source_target_pairs={{0,4},{4,0},{1,5},{5,1},{2,6},{6,2},{3,7},{7,3}} | collective-permute-start | bytes 6291464 | tf_op jit(solution)/shard_map/ppermute | solution.py:584
  1609.7 295.6 %collective-permute-start.49 = (bf16[1024,3584]{1,0:T(8,128)(2,1)}, bf16[1024,3584]{1,0:T(8,128)(2,1)}, u32[]{:S(2)}, u32[]{:S(2)}) collective-permute-start(bf16[1024,3584]{1,0:T(8,128)(2,1)} %pad_maximum_fusion.2), channel_id=1, source_target_pairs={{0,2},{1,3},{2,0},{3,1},{4,6},{5,7},{6,4},{7,5}} | collective-permute-start | bytes 22020104 | tf_op jit(solution)/shard_map/ppermute | solution.py:578
  1905.4 210.1 %collective-permute-start.50 = (bf16[1024,3584]{1,0:T(8,128)(2,1)}, bf16[1024,3584]{1,0:T(8,128)(2,1)}, u32[]{:S(2)}, u32[]{:S(2)}) collective-permute-start(bf16[1024,3584]{1,0:T(8,128)(2,1)} %collective-permute-done.49.refs_5_), channel_id=1, source_target_pairs={{0,1},{1,0},{2,3},{3,2},{4,5},{5,4},{6,7},{7,6}} | collective-permute-start | bytes 22020104 | tf_op jit(solution)/shard_map/ppermute | solution.py:580
  1912.2 242.0 %collective-permute-start.51 = (bf16[1024,3584]{1,0:T(8,128)(2,1)}, bf16[1024,3584]{1,0:T(8,128)(2,1)}, u32[]{:S(2)}, u32[]{:S(2)}) collective-permute-start(bf16[1024,3584]{1,0:T(8,128)(2,1)} %pad_maximum_fusion.3), channel_id=1, source_target_pairs={{0,2},{1,3},{2,0},{3,1},{4,6},{5,7},{6,4},{7,5}} | collective-permute-start | bytes 22020104 | tf_op jit(solution)/shard_map/ppermute | solution.py:578
  1913.3 93.4 %collective-permute-start.47 = (bf16[1024,2048]{1,0:T(8,128)(2,1)S(1)}, bf16[1024,2048]{1,0:T(8,128)(2,1)S(1)}, u32[]{:S(2)}, u32[]{:S(2)}) collective-permute-start(bf16[1024,2048]{1,0:T(8,128)(2,1)S(1)} %copy-done.2), channel_id=1, source_target_pairs={{0,4},{4,0},{1,5},{5,1},{2,6},{6,2},{3,7},{7,3}} | collective-permute-start | bytes 12582920 | tf_op jit(solution)/shard_map/ppermute | solution.py:584
  1914.2 181.6 %collective-permute-start.48 = (bf16[1024,2048]{1,0:T(8,128)(2,1)}, bf16[1024,2048]{1,0:T(8,128)(2,1)S(1)}, u32[]{:S(2)}, u32[]{:S(2)}) collective-permute-start(bf16[1024,2048]{1,0:T(8,128)(2,1)} %shard_map.154.refs_2_), channel_id=1, source_target_pairs={{0,4},{4,0},{1,5},{5,1},{2,6},{6,2},{3,7},{7,3}} | collective-permute-start | bytes 12582920 | tf_op jit(solution)/shard_map/ppermute | solution.py:584
  2168.6 93.8 %collective-permute-start.54 = (bf16[1024,2048]{1,0:T(8,128)(2,1)}, bf16[1024,2048]{1,0:T(8,128)(2,1)}, u32[]{:S(2)}, u32[]{:S(2)}) collective-permute-start(bf16[1024,2048]{1,0:T(8,128)(2,1)} %shard_map.158.refs_2_), channel_id=1, source_target_pairs={{0,4},{4,0},{1,5},{5,1},{2,6},{6,2},{3,7},{7,3}} | collective-permute-start | bytes 12582920 | tf_op jit(solution)/shard_map/ppermute | solution.py:584
  2169.5 182.2 %collective-permute-start.53 = (bf16[1024,2048]{1,0:T(8,128)(2,1)}, bf16[1024,2048]{1,0:T(8,128)(2,1)}, u32[]{:S(2)}, u32[]{:S(2)}) collective-permute-start(bf16[1024,2048]{1,0:T(8,128)(2,1)} %shard_map.157.refs_1_), channel_id=1, source_target_pairs={{0,4},{4,0},{1,5},{5,1},{2,6},{6,2},{3,7},{7,3}} | collective-permute-start | bytes 12582920 | tf_op jit(solution)/shard_map/ppermute | solution.py:584
  2175.7 270.3 %collective-permute-start.55 = (bf16[1024,3072]{1,0:T(8,128)(2,1)}, bf16[1024,3072]{1,0:T(8,128)(2,1)}, u32[]{:S(2)}, u32[]{:S(2)}) collective-permute-start(bf16[1024,3072]{1,0:T(8,128)(2,1)} %pad_maximum_fusion.5), channel_id=1, source_target_pairs={{0,2},{1,3},{2,0},{3,1},{4,6},{5,7},{6,4},{7,5}} | collective-permute-start | bytes 18874376 | tf_op jit(solution)/shard_map/ppermute | solution.py:578
  2452.1 93.3 %collective-permute-start.57 = (bf16[1024,2048]{1,0:T(8,128)(2,1)}, bf16[1024,2048]{1,0:T(8,128)(2,1)}, u32[]{:S(2)}, u32[]{:S(2)}) collective-permute-start(bf16[1024,2048]{1,0:T(8,128)(2,1)} %pad_maximum_fusion.7), channel_id=1, source_target_pairs={{0,2},{1,3},{2,0},{3,1},{4,6},{5,7},{6,4},{7,5}} | collective-permute-start | bytes 12582920 | tf_op jit(solution)/shard_map/ppermute | solution.py:578
  2545.4 138.2 %collective-permute-start.59 = (bf16[6144,512]{1,0:T(8,128)(2,1)}, bf16[6144,512]{1,0:T(8,128)(2,1)}, u32[]{:S(2)}, u32[]{:S(2)}) collective-permute-start(bf16[6144,512]{1,0:T(8,128)(2,1)} %get-tuple-element.214), channel_id=1, source_target_pairs={{0,2},{1,3},{2,0},{3,1},{4,6},{5,7},{6,4},{7,5}} | collective-permute-start | bytes 18874376 | tf_op jit(solution)/shard_map/ppermute | solution.py:578
  2683.6 138.2 %collective-permute-start.61 = (bf16[6144,512]{1,0:T(8,128)(2,1)}, bf16[6144,512]{1,0:T(8,128)(2,1)}, u32[]{:S(2)}, u32[]{:S(2)}) collective-permute-start(bf16[6144,512]{1,0:T(8,128)(2,1)} %get-tuple-element.218), channel_id=1, source_target_pairs={{0,2},{1,3},{2,0},{3,1},{4,6},{5,7},{6,4},{7,5}} | collective-permute-start | bytes 18874376 | tf_op jit(solution)/shard_map/ppermute | solution.py:578
  2827.7 210.5 %collective-permute-start.66 = (bf16[1024,1024]{1,0:T(8,128)(2,1)}, bf16[1024,1024]{1,0:T(8,128)(2,1)}, u32[]{:S(2)}, u32[]{:S(2)}) collective-permute-start(bf16[1024,1024]{1,0:T(8,128)(2,1)} %shard_map.172.p_ref), channel_id=1, source_target_pairs={{0,4},{4,0},{1,5},{5,1},{2,6},{6,2},{3,7},{7,3}} | collective-permute-start | bytes 6291464 | tf_op jit(solution)/shard_map/ppermute | solution.py:584
  2828.6 92.8 %collective-permute-start.64 = (bf16[1024,1024]{1,0:T(8,128)(2,1)}, bf16[1024,1024]{1,0:T(8,128)(2,1)}, u32[]{:S(2)}, u32[]{:S(2)}) collective-permute-start(bf16[1024,1024]{1,0:T(8,128)(2,1)} %shard_map.171.p_ref), channel_id=1, source_target_pairs={{0,4},{4,0},{1,5},{5,1},{2,6},{6,2},{3,7},{7,3}} | collective-permute-start | bytes 6291464 | tf_op jit(solution)/shard_map/ppermute | solution.py:584
  2829.7 136.7 %collective-permute-start.65 = (bf16[1024,1024]{1,0:T(8,128)(2,1)}, bf16[1024,1024]{1,0:T(8,128)(2,1)}, u32[]{:S(2)}, u32[]{:S(2)}) collective-permute-start(bf16[1024,1024]{1,0:T(8,128)(2,1)} %shard_map.169.p_ref), channel_id=1, source_target_pairs={{0,4},{4,0},{1,5},{5,1},{2,6},{6,2},{3,7},{7,3}} | collective-permute-start | bytes 6291464 | tf_op jit(solution)/shard_map/ppermute | solution.py:584
  2830.6 180.7 %collective-permute-start.63 = (bf16[1024,1024]{1,0:T(8,128)(2,1)}, bf16[1024,1024]{1,0:T(8,128)(2,1)}, u32[]{:S(2)}, u32[]{:S(2)}) collective-permute-start(bf16[1024,1024]{1,0:T(8,128)(2,1)} %shard_map.168.p_ref), channel_id=1, source_target_pairs={{0,4},{4,0},{1,5},{5,1},{2,6},{6,2},{3,7},{7,3}} | collective-permute-start | bytes 6291464 | tf_op jit(solution)/shard_map/ppermute | solution.py:584
  2832.4 274.5 %collective-permute-start.68 = (bf16[1024,1024]{1,0:T(8,128)(2,1)}, bf16[1024,1024]{1,0:T(8,128)(2,1)}, u32[]{:S(2)}, u32[]{:S(2)}) collective-permute-start(bf16[1024,1024]{1,0:T(8,128)(2,1)} %shard_map.174.p_ref), channel_id=1, source_target_pairs={{0,4},{4,0},{1,5},{5,1},{2,6},{6,2},{3,7},{7,3}} | collective-permute-start | bytes 6291464 | tf_op jit(solution)/shard_map/ppermute | solution.py:584
  2921.4 179.8 %collective-permute-start.67 = (bf16[1024,1024]{1,0:T(8,128)(2,1)}, bf16[1024,1024]{1,0:T(8,128)(2,1)}, u32[]{:S(2)}, u32[]{:S(2)}) collective-permute-start(bf16[1024,1024]{1,0:T(8,128)(2,1)} %shard_map.173.p_ref), channel_id=1, source_target_pairs={{0,4},{4,0},{1,5},{5,1},{2,6},{6,2},{3,7},{7,3}} | collective-permute-start | bytes 6291464 | tf_op jit(solution)/shard_map/ppermute | solution.py:584
  2966.4 179.8 %collective-permute-start.69 = (bf16[1024,1024]{1,0:T(8,128)(2,1)}, bf16[1024,1024]{1,0:T(8,128)(2,1)}, u32[]{:S(2)}, u32[]{:S(2)}) collective-permute-start(bf16[1024,1024]{1,0:T(8,128)(2,1)} %shard_map.175.p_ref), channel_id=1, source_target_pairs={{0,4},{4,0},{1,5},{5,1},{2,6},{6,2},{3,7},{7,3}} | collective-permute-start | bytes 6291464 | tf_op jit(solution)/shard_map/ppermute | solution.py:584
  3011.3 179.3 %collective-permute-start.70 = (bf16[1024,1024]{1,0:T(8,128)(2,1)}, bf16[1024,1024]{1,0:T(8,128)(2,1)}, u32[]{:S(2)}, u32[]{:S(2)}) collective-permute-start(bf16[1024,1024]{1,0:T(8,128)(2,1)} %shard_map.176.p_ref), channel_id=1, source_target_pairs={{0,4},{4,0},{1,5},{5,1},{2,6},{6,2},{3,7},{7,3}} | collective-permute-start | bytes 6291464 | tf_op jit(solution)/shard_map/ppermute | solution.py:584
  (41 other events, 937.3 us)

commit v2 on v1

--- a/solution.py
+++ b/solution.py
@@ -12,23 +12,24 @@
 ROPE_THETA = 1.0e6
 NORM_EPS = 1.0e-5
 LOG2E = 1.4426950408889634
-GU_BLOCKS = (7, 7, 6, 4)
+GU_BLOCKS = (7, 7, 5, 3, 2)
 GU_BN = 256
 
 X, C, N, Y, K = "x", "c", "n", "y", "K"
 G, Q, KV, O, GU, D, GATE, UP, DOWN = "g", "q", "kv", "o", "gu", "d", "gate", "up", "down"
-I0, I1, I2, I3 = range(4)
-FIRST, QKV, ATTN, OA, OB, ADDO, DA, DC, ADDM, LAST = "first", "qkv", "attn", "oa", "ob", "addo", "da", "dc", "addm", "last"
+I0, I1, I2, I3, I4 = range(5)
+FIRST, QKV, ATTN, OA, OB, ADDO = "first", "qkv", "attn", "oa", "ob", "addo"
+DA, DB, DC, ADDM, LAST = "da", "db", "dc", "addm", "last"
 
 PLAN = (
-    (X, Q, I0), (N, Q, I0), (X, G), (N, G), (X, KV, I0), (N, KV, I0), (X, O, I0), (C, G), (X, GU, I0, I0),
-    (X, GU, I0, I1), (N, O),
+    (X, Q, I0), (N, Q, I0), (X, G), (N, G), (X, KV, I0), (N, KV, I0), (X, O, I0), (C, G), (X, GU, I0, I0), (X, GU, I0, I1),
+    (N, O),
     (K, FIRST, I0), (K, FIRST, I1),
     (C, Q, I0), (C, KV, I0), (X, GU, I0, I2),
     (K, QKV, I0, I0), (K, ATTN, I0, I0),
-    (C, O, I0), (X, GU, I0, I3), (N, GATE), (N, UP),
-    (K, OA, I0, I0), (Y, OA, I0, I0), (K, OB, I0, I0), (Y, OB, I0, I0), (K, QKV, I0, I1), (K, ATTN, I0, I1), (K, OA, I0, I1),
-    (Y, OA, I0, I1), (K, OB, I0, I1), (Y, OB, I0, I1),
+    (C, O, I0), (X, GU, I0, I3), (X, GU, I0, I4), (N, GATE), (N, UP),
+    (K, OA, I0, I0), (Y, OA, I0, I0), (K, OB, I0, I0), (Y, OB, I0, I0), (K, QKV, I0, I1), (K, ATTN, I0, I1),
+    (K, OA, I0, I1), (Y, OA, I0, I1), (K, OB, I0, I1), (Y, OB, I0, I1),
     (C, GU, I0, I0), (X, D, I0, I0), (N, DOWN),
     (K, ADDO, I0, I0), (K, GU, I0, I0, I0),
     (C, GU, I0, I1), (X, D, I0, I1),
@@ -36,37 +37,39 @@
     (C, GU, I0, I2), (X, Q, I1), (X, KV, I1),
     (K, GU, I0, I1, I1), (K, GU, I0, I2, I0),
     (C, GU, I0, I3), (X, O, I1), (N, Q, I1), (N, KV, I1),
-    (K, GU, I0, I2, I1), (K, GU, I0, I3, I0), (K, DA, I0, I0), (Y, DA, I0, I0), (K, DC, I0, I0), (Y, DC, I0, I0),
-    (K, GU, I0, I3, I1),
-    (K, DA, I0, I1), (Y, DA, I0, I1),
-    (C, D, I0, I0), (X, GU, I1, I0),
+    (K, GU, I0, I2, I1),
+    (C, GU, I0, I4), (X, GU, I1, I0),
+    (K, GU, I0, I3, I0), (K, GU, I0, I4, I0), (K, DA, I0, I0), (Y, DA, I0, I0), (K, DB, I0, I0), (Y, DB, I0, I0),
+    (K, DC, I0, I0), (Y, DC, I0, I0), (K, GU, I0, I3, I1), (K, GU, I0, I4, I1), (K, DA, I0, I1), (Y, DA, I0, I1),
+    (K, DB, I0, I1), (Y, DB, I0, I1),
+    (C, D, I0, I0), (X, GU, I1, I1),
     (K, DC, I0, I1), (Y, DC, I0, I1), (K, D, I0, I0, I0), (Y, D, I0, I0, I0),
-    (C, D, I0, I1), (X, GU, I1, I1),
-    (K, D, I1, I0, I0), (Y, D, I1, I0, I0), (K, D, I0, I0, I1), (Y, D, I0, I0, I1), (K, D, I1, I0, I1),
-    (Y, D, I1, I0, I1), (K, ADDM, I0, I0),
-    (C, Q, I1), (C, KV, I1), (X, GU, I1, I2),
+    (C, D, I0, I1), (X, GU, I1, I2),
+    (K, D, I1, I0, I0), (Y, D, I1, I0, I0), (K, D, I0, I0, I1), (Y, D, I0, I0, I1), (K, D, I1, I0, I1), (Y, D, I1, I0, I1),
+    (K, ADDM, I0, I0),
+    (C, Q, I1), (C, KV, I1), (X, GU, I1, I3), (X, GU, I1, I4),
     (K, QKV, I1, I0), (K, ATTN, I1, I0), (K, OA, I1, I0), (Y, OA, I1, I0),
-    (C, O, I1), (X, GU, I1, I3),
+    (C, O, I1), (X, D, I1, I0),
     (K, ADDM, I0, I1), (K, OB, I1, I0), (Y, OB, I1, I0), (K, QKV, I1, I1), (K, ATTN, I1, I1), (K, OA, I1, I1),
-    (Y, OA, I1, I1),
-    (K, OB, I1, I1), (Y, OB, I1, I1),
-    (C, GU, I1, I0), (X, D, I1, I0),
+    (Y, OA, I1, I1), (K, OB, I1, I1), (Y, OB, I1, I1),
+    (C, GU, I1, I0), (X, D, I1, I1),
     (K, ADDO, I1, I0), (K, GU, I1, I0, I0),
-    (C, GU, I1, I1), (X, D, I1, I1),
-    (K, GU, I1, I1, I0), (K, ADDO, I1, I1), (K, GU, I1, I0, I1), (K, GU, I1, I1, I1),
+    (C, GU, I1, I1),
+    (K, GU, I1, I1, I0), (K, ADDO, I1, I1), (K, GU, I1, I0, I1),
     (C, GU, I1, I2),
-    (K, GU, I1, I2, I0), (K, GU, I1, I2, I1),
+    (K, GU, I1, I1, I1), (K, GU, I1, I2, I0),
     (C, GU, I1, I3),
-    (K, GU, I1, I3, I0), (K, DA, I1, I0), (Y, DA, I1, I0), (K, DC, I1, I0), (Y, DC, I1, I0), (K, GU, I1, I3, I1),
-    (K, DA, I1, I1),
-    (Y, DA, I1, I1), (K, DC, I1, I1), (Y, DC, I1, I1),
+    (K, GU, I1, I2, I1), (K, GU, I1, I3, I0),
+    (C, GU, I1, I4),
+    (K, GU, I1, I4, I0), (K, DA, I1, I0), (Y, DA, I1, I0), (K, DB, I1, I0), (Y, DB, I1, I0), (K, DC, I1, I0),
+    (Y, DC, I1, I0), (K, GU, I1, I3, I1), (K, GU, I1, I4, I1), (K, DA, I1, I1), (Y, DA, I1, I1), (K, DB, I1, I1),
+    (Y, DB, I1, I1), (K, DC, I1, I1), (Y, DC, I1, I1),
     (C, D, I1, I0),
     (K, D, I0, I1, I0), (Y, D, I0, I1, I0), (K, D, I0, I1, I1), (Y, D, I0, I1, I1),
     (C, D, I1, I1),
     (K, D, I1, I1, I0), (Y, D, I1, I1, I0), (K, D, I1, I1, I1), (Y, D, I1, I1, I1),
     (K, LAST, I0, I0), (K, LAST, I0, I1), (K, LAST, I1, I0), (K, LAST, I1, I1), (K, LAST, I2, I0), (K, LAST, I2, I1),
-    (K, LAST, I3, I0),
-    (K, LAST, I3, I1),
+    (K, LAST, I3, I0), (K, LAST, I3, I1), (K, LAST, I4, I0), (K, LAST, I4, I1),
 )
 
 VMEM_BYTES = 62 * 1024 * 1024
@@ -495,7 +498,7 @@
                 own[name_of(D, l, i)] = w_down[l][:, i * dw:(i + 1) * dw]
 
         seg_a = [(0, 0, quarter), (quarter, quarter, quarter)]
-        seg_own, seg_core = [(0, 0, quarter)], [(0, quarter, quarter)]
+        seg_own, seg_core = [[(0, 0, dw)], [(0, dw, dw)]], [(0, quarter, quarter)]
         seg_b = [(0, 2 * quarter, quarter), (quarter, 3 * quarter, quarter)]
         seg_d = [[(0, 2 * quarter + i * dw, dw), (dw, 3 * quarter + i * dw, dw)] for i in range(2)]
 
@@ -507,7 +510,7 @@
             return [own[key], nr[key], xr[key], cr[key]]
 
         def kernel(name, dep, op, *idx):
-            s, l = idx[-1], idx[-2] if op in (D, QKV, ATTN, OA, OB, ADDO, DA, DC, ADDM) else idx[0]
+            s, l = idx[-1], idx[-2] if op in (D, QKV, ATTN, OA, OB, ADDO, DA, DB, DC, ADDM) else idx[0]
             if op == FIRST:
                 if not gains:
                     rows = jnp.concatenate(pieces(G), axis=1).astype(F32)
@@ -526,9 +529,10 @@
                 plan = [(0, l, 0), (0, l, dw), (1, l, 0), (1, l, dw)]
                 part[name] = cols_call(dep(ctx[s]), [w_o, nr[O]], plan, dw)
                 return part[name]
-            if op in (DA, DC):
-                w = w_down if op == DA else nr[DOWN]
-                part[name] = cols_call(dep(acts[s]), [w], [(0, l, 0), (0, l, dw)], dw)
+            if op in (DA, DB, DC):
+                w = nr[DOWN] if op == DC else w_down
+                plan = [(0, l, 0), (0, l, dw)] if op == DC else [(0, l, dw if op == DB else 0)]
+                part[name] = cols_call(dep(acts[s]), [w], plan, dw)
                 return part[name]
             if op == OB:
                 key = name_of(O, l)
@@ -551,8 +555,8 @@
                 hid[s], hn[s] = add_call(dep(hid[s]), units, gains[n_layers + l])
                 return hn[s]
             last_l = l if op == ADDM else n_layers - 1
-            tags = [name_of(DA, last_l, s), name_of(DC, last_l, s), name_of(D, 0, last_l, s), name_of(D, 1, last_l, s)]
-            segs = [seg_own, seg_core] + seg_d
+            tags = [name_of(w, last_l, s) for w in (DA, DB, DC)] + [name_of(D, i, last_l, s) for i in range(2)]
+            segs = seg_own + [seg_core] + seg_d
             if op == ADDM:
                 units = [(part[t], yr[t], g) for t, g in zip(tags, segs)]
                 hid[s], hn[s] = add_call(dep(hid[s]), units, gains[l + 1])

time: 3210 us -> 3260 us (1.016)
  Pallas kernels: 1490 us -> 1540 us
    pallas_call x24 -> x28, Pallas kernels: 422 us -> 444 us  [cols_call(): pl.pallas_call(functools.partial(cols_body, plan=plan, n_w=len(ws), tm=tm...]
    pallas_call x16 -> x20, Pallas kernels: 540 us -> 561 us  [gu_call(): pl.pallas_call(functools.partial(gu_body, bn=bn, base=first * bn, tm=tm,...]
    ppermute x19 -> x21, waiting for transfers between devices: 334 us -> 343 us  [device_fn(): xr[name] = lax.ppermute(dep(own[name]), 'fsdp', far)]
    ppermute x24 -> x28, waiting for transfers between devices: 1100 us -> 1090 us  [device_fn(): yr[name] = lax.ppermute(part[name], 'tp', swap)]
  transfers between devices with their start and end apart: 71 -> 79, of which waited for: 36 -> 31; matrix products, arithmetic and copies ran while one was open for 5% -> 5% of each run, Pallas kernels for 46% -> 47%
where the time goes in v2:
time: 3260 us; the launch traced here: 3250 us
  Pallas kernels  1540 us (47%)
  waiting for transfers between devices  1450 us (44%)
  local copies, waits for them, and re-layouts  134 us (4%)
  starting transfers between devices  62.3 us (2%)
  other arithmetic  57.1 us (2%)
    ppermute x28, waiting for transfers between devices, device_fn(): yr[name] = lax.ppermute(part[name], 'tp', swap)  1090 us
    pallas_call x20, Pallas kernels, gu_call(): pl.pallas_call(functools.partial(gu_body, bn=bn, base=first * bn, tm=tm,...  561 us
    pallas_call x28, Pallas kernels, cols_call(): pl.pallas_call(functools.partial(cols_body, plan=plan, n_w=len(ws), tm=tm...  444 us
    ppermute x21, waiting for transfers between devices, device_fn(): xr[name] = lax.ppermute(dep(own[name]), 'fsdp', far)  343 us
    pallas_call x4, Pallas kernels, attn_call(): pl.pallas_call(functools.partial(attn_body, n_past=len(past), bq=256, sca...  199 us
    pallas_call x4, Pallas kernels, qkv_call(): pl.pallas_call(functools.partial(qkv_body, bn=bn, n_rope=rope_cols // bn,...  155 us
    pallas_call x6, Pallas kernels, add_call(): pl.pallas_call(functools.partial(add_body, segs=segs), grid=(t // tb,), i...  106 us
  transfers between devices with their start and end apart: 79, of which 31 were waited for; matrix products, arithmetic and copies ran while one was open for 5% of the time, Pallas kernels for 47%

profile of v2, /device:TPU:0, one launch (start us, length us, event | category | flops | bytes accessed | tf_op | source)
XLA Modules:
  0.0 3246.1 jit_solution(15559039017364834820)
XLA Ops:
  13.2 87.5 %collective-permute-done.1 = bf16[4,1024]{1,0:T(4,128)(2,1)S(1)} collective-permute-done((bf16[4,1024]{1,0:T(4,128)(2,1)S(1)}, bf16[4,1024]{1,0:T(4,128)(2,1)S(1)}, u32[]{:S(2)}, u32[]{:S(2)}) %collective-permute-start.1) | collective-permute-done | bytes 8224 | tf_op jit(solution)/shard_map/ppermute | solution.py:582
  170.5 38.9 %shard_map.123.q_ref.refs_0_.refs_1_.refs_2_ = bf16[1024,3072]{1,0:T(8,128)(2,1)} custom-call(bf16[1024,4096]{1,0:T(8,128)(2,1)} %get-tuple-element.135.a_hbm, f32[1024,128]{1,0:T(8,128)} %get-tuple-element.299.cos_ref, f32[1024,128]{1,0:T(8,128)} %get-tuple-element.289.sin_ref, bf16[1024,2048]{1,0:T(8,128)(2,1)} %slice_bitcast_fusion.9.refs_0_, ...), custom_call_target="tpu_custom_call" | custom-call | flops 25769803776 | bytes 39845888 | tf_op jit(solution)/shard_map/pallas_call | solution.py:177
  209.4 36.1 %shard_map.124.refs_0_ = bf16[1024,2048]{1,0:T(8,128)(2,1)} custom-call(bf16[1024,3072]{1,0:T(8,128)(2,1)} %shard_map.123.q_ref.refs_0_.refs_1_.refs_2_, bf16[1024,3072]{1,0:T(8,128)(2,1)} %shard_map.123.q_ref.refs_0_.refs_1_.refs_2_, bf16[1024,3072]{1,0:T(8,128)(2,1)} %shard_map.123.q_ref.refs_0_.refs_1_.refs_2_), custom_call_target="tpu_custom_call" | custom-call | flops 17179869184 | bytes 8388608 | tf_op jit(solution)/shard_map/pallas_call | solution.py:356
  318.6 38.9 %shard_map.127.q_ref.refs_1_.refs_3_ = bf16[1024,3072]{1,0:T(8,128)(2,1)} custom-call(bf16[1024,4096]{1,0:T(8,128)(2,1)} %get-tuple-element.142.a_hbm, f32[1024,128]{1,0:T(8,128)} %get-tuple-element.300.cos_ref, f32[1024,128]{1,0:T(8,128)} %get-tuple-element.288.sin_ref, bf16[1024,2048]{1,0:T(8,128)(2,1)} %slice_bitcast_fusion.9.refs_0_, ...), custom_call_target="tpu_custom_call" | custom-call | flops 25769803776 | bytes 39845888 | tf_op jit(solution)/shard_map/pallas_call | solution.py:177
  357.5 63.3 %shard_map.128.refs_0_ = bf16[1024,2048]{1,0:T(8,128)(2,1)} custom-call(bf16[1024,3072]{1,0:T(8,128)(2,1)} %shard_map.127.q_ref.refs_1_.refs_3_, bf16[1024,3072]{1,0:T(8,128)(2,1)} %shard_map.123.q_ref.refs_0_.refs_1_.refs_2_, bf16[1024,3072]{1,0:T(8,128)(2,1)} %shard_map.127.q_ref.refs_1_.refs_3_, ...), custom_call_target="tpu_custom_call" | custom-call | flops 51539607552 | bytes 8388608 | tf_op jit(solution)/shard_map/pallas_call | solution.py:356
  458.1 91.2 %collective-permute-done.13.refs_4_ = bf16[1024,2048]{1,0:T(8,128)(2,1)S(1)} collective-permute-done((bf16[1024,2048]{1,0:T(8,128)(2,1)S(1)}, bf16[1024,2048]{1,0:T(8,128)(2,1)S(1)}, u32[]{:S(2)}, u32[]{:S(2)}) %collective-permute-start.13) | collective-permute-done | bytes 4194336 | tf_op jit(solution)/shard_map/ppermute | solution.py:588
  569.0 38.6 %shard_map.132.refs_7_ = bf16[1024,6144]{1,0:T(8,128)(2,1)} custom-call(bf16[1024,4096]{1,0:T(8,128)(2,1)} %get-tuple-element.165.refs_0_, bf16[2,1024,6144]{2,1,0:T(8,128)(2,1)} %refs_1_.61, bf16[2,1024,6144]{2,1,0:T(8,128)(2,1)} %refs_2_.39, bf16[2,1024,6144]{2,1,0:T(8,128)(2,1)} %collective-permute-done.14.refs_3_, ...), custom_call_target="tpu_custom_call" | custom-call | flops 30064771072 | bytes 41418752 | tf_op jit(solution)/shard_map/pallas_call | solution.py:246
  645.4 38.5 %shard_map.133.refs_7_ = bf16[1024,6144]{1,0:T(8,128)(2,1)} custom-call(bf16[1024,4096]{1,0:T(8,128)(2,1)} %get-tuple-element.165.refs_0_, bf16[2,1024,6144]{2,1,0:T(8,128)(2,1)} %refs_1_.61, bf16[2,1024,6144]{2,1,0:T(8,128)(2,1)} %refs_2_.39, bf16[2,1024,6144]{2,1,0:T(8,128)(2,1)} %collective-permute-done.14.refs_3_, ...), custom_call_target="tpu_custom_call", output_to_operand_aliasing={{}: (7, {})} | custom-call | flops 30064771072 | bytes 41418752 | tf_op jit(solution)/shard_map/pallas_call | solution.py:246
  683.8 47.1 %collective-permute-done.21.refs_4_ = bf16[1024,2048]{1,0:T(8,128)(2,1)} collective-permute-done((bf16[1024,2048]{1,0:T(8,128)(2,1)}, bf16[1024,2048]{1,0:T(8,128)(2,1)}, u32[]{:S(2)}, u32[]{:S(2)}) %collective-permute-start.21) | collective-permute-done | bytes 4194336 | tf_op jit(solution)/shard_map/ppermute | solution.py:588
  730.9 88.9 %collective-permute-done.20.refs_3_ = bf16[1024,2048]{1,0:T(8,128)(2,1)} collective-permute-done((bf16[1024,2048]{1,0:T(8,128)(2,1)}, bf16[1024,2048]{1,0:T(8,128)(2,1)}, u32[]{:S(2)}, u32[]{:S(2)}) %collective-permute-start.20) | collective-permute-done | bytes 4194336 | tf_op jit(solution)/shard_map/ppermute | solution.py:588
  837.5 38.4 %shard_map.135.refs_7_ = bf16[1024,6144]{1,0:T(8,128)(2,1)} custom-call(bf16[1024,4096]{1,0:T(8,128)(2,1)} %get-tuple-element.172.refs_0_, bf16[2,1024,6144]{2,1,0:T(8,128)(2,1)} %refs_1_.61, bf16[2,1024,6144]{2,1,0:T(8,128)(2,1)} %refs_2_.39, bf16[2,1024,6144]{2,1,0:T(8,128)(2,1)} %collective-permute-done.14.refs_3_, ...), custom_call_target="tpu_custom_call" | custom-call | flops 30064771072 | bytes 41418752 | tf_op jit(solution)/shard_map/pallas_call | solution.py:246
  890.3 38.5 %shard_map.136.refs_7_ = bf16[1024,6144]{1,0:T(8,128)(2,1)} custom-call(bf16[1024,4096]{1,0:T(8,128)(2,1)} %get-tuple-element.172.refs_0_, bf16[2,1024,6144]{2,1,0:T(8,128)(2,1)} %refs_1_.61, bf16[2,1024,6144]{2,1,0:T(8,128)(2,1)} %refs_2_.39, bf16[2,1024,6144]{2,1,0:T(8,128)(2,1)} %collective-permute-done.14.refs_3_, ...), custom_call_target="tpu_custom_call", output_to_operand_aliasing={{}: (7, {})} | custom-call | flops 30064771072 | bytes 41418752 | tf_op jit(solution)/shard_map/pallas_call | solution.py:246
  928.8 29.0 shard_map.137.refs_7_
  962.5 29.3 shard_map.138.refs_7_
  1017.0 19.5 shard_map.139.refs_7_
  1095.5 19.6 shard_map.144.refs_7_
  1195.0 98.4 %collective-permute-done.31.refs_1_ = bf16[6144,512]{1,0:T(8,128)(2,1)} collective-permute-done((bf16[6144,512]{1,0:T(8,128)(2,1)}, bf16[6144,512]{1,0:T(8,128)(2,1)}, u32[]{:S(2)}, u32[]{:S(2)}) %collective-permute-start.31) | collective-permute-done | bytes 6291488 | tf_op jit(solution)/shard_map/ppermute | solution.py:582
  1344.5 19.5 shard_map.152.refs_5_
  1364.1 113.1 %collective-permute-done.33.refs_6_ = bf16[1024,512]{1,0:T(8,128)(2,1)} collective-permute-done((bf16[1024,512]{1,0:T(8,128)(2,1)S(1)}, bf16[1024,512]{1,0:T(8,128)(2,1)}, u32[]{:S(2)}, u32[]{:S(2)}) %collective-permute-start.33) | collective-permute-done | bytes 1048608 | tf_op jit(solution)/shard_map/ppermute | solution.py:588
  1496.5 29.1 collective-permute-done.42.refs_6_
  1530.1 38.8 %shard_map.154.q_ref.refs_0_.refs_1_.refs_2_ = bf16[1024,3072]{1,0:T(8,128)(2,1)} custom-call(bf16[1024,4096]{1,0:T(8,128)(2,1)} %get-tuple-element.186.a_hbm, f32[1024,128]{1,0:T(8,128)} %get-tuple-element.299.cos_ref, f32[1024,128]{1,0:T(8,128)} %get-tuple-element.289.sin_ref, bf16[1024,2048]{1,0:T(8,128)(2,1)} %slice_bitcast_fusion.7.refs_0_, ...), custom_call_target="tpu_custom_call" | custom-call | flops 25769803776 | bytes 39845888 | tf_op jit(solution)/shard_map/pallas_call | solution.py:177
  1568.9 36.0 %shard_map.155.refs_0_ = bf16[1024,2048]{1,0:T(8,128)(2,1)} custom-call(bf16[1024,3072]{1,0:T(8,128)(2,1)} %shard_map.154.q_ref.refs_0_.refs_1_.refs_2_, bf16[1024,3072]{1,0:T(8,128)(2,1)} %shard_map.154.q_ref.refs_0_.refs_1_.refs_2_, bf16[1024,3072]{1,0:T(8,128)(2,1)} %shard_map.154.q_ref.refs_0_.refs_1_.refs_2_), custom_call_target="tpu_custom_call" | custom-call | flops 17179869184 | bytes 8388608 | tf_op jit(solution)/shard_map/pallas_call | solution.py:356
  1623.3 22.2 collective-permute-done.45.refs_7_
  1646.4 155.7 %collective-permute-done.44.refs_6_ = bf16[1024,512]{1,0:T(8,128)(2,1)S(1)} collective-permute-done((bf16[1024,512]{1,0:T(8,128)(2,1)S(1)}, bf16[1024,512]{1,0:T(8,128)(2,1)S(1)}, u32[]{:S(2)}, u32[]{:S(2)}) %collective-permute-start.44) | collective-permute-done | bytes 1048608 | tf_op jit(solution)/shard_map/ppermute | solution.py:588
  1835.0 38.8 %shard_map.159.q_ref.refs_1_.refs_3_ = bf16[1024,3072]{1,0:T(8,128)(2,1)} custom-call(bf16[1024,4096]{1,0:T(8,128)(2,1)} %get-tuple-element.203.a_hbm, f32[1024,128]{1,0:T(8,128)} %get-tuple-element.300.cos_ref, f32[1024,128]{1,0:T(8,128)} %get-tuple-element.288.sin_ref, bf16[1024,2048]{1,0:T(8,128)(2,1)} %slice_bitcast_fusion.7.refs_0_, ...), custom_call_target="tpu_custom_call" | custom-call | flops 25769803776 | bytes 39845888 | tf_op jit(solution)/shard_map/pallas_call | solution.py:177
  1873.9 63.7 %shard_map.160.refs_0_ = bf16[1024,2048]{1,0:T(8,128)(2,1)} custom-call(bf16[1024,3072]{1,0:T(8,128)(2,1)} %shard_map.159.q_ref.refs_1_.refs_3_, bf16[1024,3072]{1,0:T(8,128)(2,1)} %shard_map.154.q_ref.refs_0_.refs_1_.refs_2_, bf16[1024,3072]{1,0:T(8,128)(2,1)} %shard_map.159.q_ref.refs_1_.refs_3_, ...), custom_call_target="tpu_custom_call" | custom-call | flops 51539607552 | bytes 8388608 | tf_op jit(solution)/shard_map/pallas_call | solution.py:356
  1975.3 91.4 %collective-permute-done.51.refs_3_ = bf16[1024,2048]{1,0:T(8,128)(2,1)S(1)} collective-permute-done((bf16[1024,2048]{1,0:T(8,128)(2,1)S(1)}, bf16[1024,2048]{1,0:T(8,128)(2,1)S(1)}, u32[]{:S(2)}, u32[]{:S(2)}) %collective-permute-start.51) | collective-permute-done | bytes 4194336 | tf_op jit(solution)/shard_map/ppermute | solution.py:588
  2068.8 87.1 %collective-permute-done.52.refs_4_ = bf16[1024,2048]{1,0:T(8,128)(2,1)S(1)} collective-permute-done((bf16[1024,2048]{1,0:T(8,128)(2,1)}, bf16[1024,2048]{1,0:T(8,128)(2,1)S(1)}, u32[]{:S(2)}, u32[]{:S(2)}) %collective-permute-start.52) | collective-permute-done | bytes 4194336 | tf_op jit(solution)/shard_map/ppermute | solution.py:588
  2175.6 38.4 %shard_map.164.refs_7_ = bf16[1024,6144]{1,0:T(8,128)(2,1)} custom-call(bf16[1024,4096]{1,0:T(8,128)(2,1)} %get-tuple-element.228.refs_0_, bf16[2,1024,6144]{2,1,0:T(8,128)(2,1)} %refs_1_.61, bf16[2,1024,6144]{2,1,0:T(8,128)(2,1)} %refs_2_.39, bf16[2,1024,6144]{2,1,0:T(8,128)(2,1)} %collective-permute-done.14.refs_3_, ...), custom_call_target="tpu_custom_call" | custom-call | flops 30064771072 | bytes 41418752 | tf_op jit(solution)/shard_map/pallas_call | solution.py:246
  2226.1 38.4 %shard_map.165.refs_7_ = bf16[1024,6144]{1,0:T(8,128)(2,1)} custom-call(bf16[1024,4096]{1,0:T(8,128)(2,1)} %get-tuple-element.228.refs_0_, bf16[2,1024,6144]{2,1,0:T(8,128)(2,1)} %refs_1_.61, bf16[2,1024,6144]{2,1,0:T(8,128)(2,1)} %refs_2_.39, bf16[2,1024,6144]{2,1,0:T(8,128)(2,1)} %collective-permute-done.14.refs_3_, ...), custom_call_target="tpu_custom_call", output_to_operand_aliasing={{}: (7, {})} | custom-call | flops 30064771072 | bytes 41418752 | tf_op jit(solution)/shard_map/pallas_call | solution.py:246
  2264.5 43.4 %collective-permute-done.58.refs_4_ = bf16[1024,2048]{1,0:T(8,128)(2,1)} collective-permute-done((bf16[1024,2048]{1,0:T(8,128)(2,1)}, bf16[1024,2048]{1,0:T(8,128)(2,1)}, u32[]{:S(2)}, u32[]{:S(2)}) %collective-permute-start.58) | collective-permute-done | bytes 4194336 | tf_op jit(solution)/shard_map/ppermute | solution.py:588
  2307.9 89.4 %collective-permute-done.57.refs_3_ = bf16[1024,2048]{1,0:T(8,128)(2,1)} collective-permute-done((bf16[1024,2048]{1,0:T(8,128)(2,1)}, bf16[1024,2048]{1,0:T(8,128)(2,1)}, u32[]{:S(2)}, u32[]{:S(2)}) %collective-permute-start.57) | collective-permute-done | bytes 4194336 | tf_op jit(solution)/shard_map/ppermute | solution.py:588
  2414.8 38.5 %shard_map.167.refs_7_ = bf16[1024,6144]{1,0:T(8,128)(2,1)} custom-call(bf16[1024,4096]{1,0:T(8,128)(2,1)} %get-tuple-element.235.refs_0_, bf16[2,1024,6144]{2,1,0:T(8,128)(2,1)} %refs_1_.61, bf16[2,1024,6144]{2,1,0:T(8,128)(2,1)} %refs_2_.39, bf16[2,1024,6144]{2,1,0:T(8,128)(2,1)} %collective-permute-done.14.refs_3_, ...), custom_call_target="tpu_custom_call" | custom-call | flops 30064771072 | bytes 41418752 | tf_op jit(solution)/shard_map/pallas_call | solution.py:246
  2459.4 38.3 %shard_map.168.refs_7_ = bf16[1024,6144]{1,0:T(8,128)(2,1)} custom-call(bf16[1024,4096]{1,0:T(8,128)(2,1)} %get-tuple-element.235.refs_0_, bf16[2,1024,6144]{2,1,0:T(8,128)(2,1)} %refs_1_.61, bf16[2,1024,6144]{2,1,0:T(8,128)(2,1)} %refs_2_.39, bf16[2,1024,6144]{2,1,0:T(8,128)(2,1)} %collective-permute-done.14.refs_3_, ...), custom_call_target="tpu_custom_call", output_to_operand_aliasing={{}: (7, {})} | custom-call | flops 30064771072 | bytes 41418752 | tf_op jit(solution)/shard_map/pallas_call | solution.py:246
  2497.8 29.0 shard_map.169.refs_7_
  2534.4 28.9 shard_map.170.refs_7_
  2563.3 19.6 shard_map.171.refs_7_
  2634.0 19.5 shard_map.175.p_ref
  2653.5 19.5 shard_map.176.refs_7_
  2742.6 19.5 shard_map.181.p_ref
  2781.5 88.9 %collective-permute-done.67.refs_1_ = bf16[6144,512]{1,0:T(8,128)(2,1)} collective-permute-done((bf16[6144,512]{1,0:T(8,128)(2,1)}, bf16[6144,512]{1,0:T(8,128)(2,1)}, u32[]{:S(2)}, u32[]{:S(2)}) %collective-permute-start.67) | collective-permute-done | bytes 6291488 | tf_op jit(solution)/shard_map/ppermute | solution.py:582
  2882.8 19.4 shard_map.183.p_ref
  2927.4 21.0 collective-permute-done.72.r_ref
  2949.9 21.0 collective-permute-done.70.r_ref
  2972.3 43.4 %collective-permute-done.73.r_ref = bf16[1024,1024]{1,0:T(8,128)(2,1)} collective-permute-done((bf16[1024,1024]{1,0:T(8,128)(2,1)}, bf16[1024,1024]{1,0:T(8,128)(2,1)}, u32[]{:S(2)}, u32[]{:S(2)}) %collective-permute-start.73) | collective-permute-done | bytes 2097184 | tf_op jit(solution)/shard_map/ppermute | solution.py:588
  3065.6 84.9 %collective-permute-done.75.r_ref = bf16[1024,1024]{1,0:T(8,128)(2,1)} collective-permute-done((bf16[1024,1024]{1,0:T(8,128)(2,1)}, bf16[1024,1024]{1,0:T(8,128)(2,1)}, u32[]{:S(2)}, u32[]{:S(2)}) %collective-permute-start.75) | collective-permute-done | bytes 2097184 | tf_op jit(solution)/shard_map/ppermute | solution.py:588
  3161.9 33.7 %collective-permute-done.77.r_ref = bf16[1024,1024]{1,0:T(8,128)(2,1)} collective-permute-done((bf16[1024,1024]{1,0:T(8,128)(2,1)}, bf16[1024,1024]{1,0:T(8,128)(2,1)}, u32[]{:S(2)}, u32[]{:S(2)}) %collective-permute-start.77) | collective-permute-done | bytes 2097184 | tf_op jit(solution)/shard_map/ppermute | solution.py:588
  3201.2 38.8 %collective-permute-done.78.r_ref = bf16[1024,1024]{1,0:T(8,128)(2,1)} collective-permute-done((bf16[1024,1024]{1,0:T(8,128)(2,1)}, bf16[1024,1024]{1,0:T(8,128)(2,1)}, u32[]{:S(2)}, u32[]{:S(2)}) %collective-permute-start.78) | collective-permute-done | bytes 2097184 | tf_op jit(solution)/shard_map/ppermute | solution.py:588
  (279 shorter events, 933.4 us)
Async XLA Ops:
  5.6 120.9 %collective-permute-start.4 = (bf16[1024,2048]{1,0:T(8,128)(2,1)}, bf16[1024,2048]{1,0:T(8,128)(2,1)}, u32[]{:S(2)}, u32[]{:S(2)}) collective-permute-start(bf16[1024,2048]{1,0:T(8,128)(2,1)} %slice_bitcast_fusion.9.refs_0_), channel_id=1, source_target_pairs={{0,2},{1,3},{2,0},{3,1},{4,6},{5,7},{6,4},{7,5}} | collective-permute-start | bytes 12582920 | tf_op jit(solution)/shard_map/ppermute | solution.py:582
  8.9 91.8 %collective-permute-start.1 = (bf16[4,1024]{1,0:T(4,128)(2,1)S(1)}, bf16[4,1024]{1,0:T(4,128)(2,1)S(1)}, u32[]{:S(2)}, u32[]{:S(2)}) collective-permute-start(bf16[4,1024]{1,0:T(4,128)(2,1)S(1)} %pad_maximum_fusion.14), channel_id=1, source_target_pairs={{0,2},{1,3},{2,0},{3,1},{4,6},{5,7},{6,4},{7,5}} | collective-permute-start | bytes 24584 | tf_op jit(solution)/shard_map/ppermute | solution.py:582
  9.0 92.4 %collective-permute-start = (bf16[4,1024]{1,0:T(4,128)(2,1)S(1)}, bf16[4,1024]{1,0:T(4,128)(2,1)S(1)}, u32[]{:S(2)}, u32[]{:S(2)}) collective-permute-start(bf16[4,1024]{1,0:T(4,128)(2,1)S(1)} %pad_maximum_fusion.14), channel_id=1, source_target_pairs={{0,1},{1,0},{2,3},{3,2},{4,5},{5,4},{6,7},{7,6}} | collective-permute-start | bytes 24584 | tf_op jit(solution)/shard_map/ppermute | solution.py:586
  9.0 160.9 %collective-permute-start.3 = (bf16[1024,2048]{1,0:T(8,128)(2,1)}, bf16[1024,2048]{1,0:T(8,128)(2,1)}, u32[]{:S(2)}, u32[]{:S(2)}) collective-permute-start(bf16[1024,2048]{1,0:T(8,128)(2,1)} %slice_bitcast_fusion.9.refs_0_), channel_id=1, source_target_pairs={{0,1},{1,0},{2,3},{3,2},{4,5},{5,4},{6,7},{7,6}} | collective-permute-start | bytes 12582920 | tf_op jit(solution)/shard_map/ppermute | solution.py:586
  11.2 134.5 %collective-permute-start.7 = (bf16[1024,1024]{1,0:T(8,128)(2,1)}, bf16[1024,1024]{1,0:T(8,128)(2,1)}, u32[]{:S(2)}, u32[]{:S(2)}) collective-permute-start(bf16[1024,1024]{1,0:T(8,128)(2,1)} %pad_maximum_fusion.8.refs_4_), channel_id=1, source_target_pairs={{0,2},{1,3},{2,0},{3,1},{4,6},{5,7},{6,4},{7,5}} | collective-permute-start | bytes 6291464 | tf_op jit(solution)/shard_map/ppermute | solution.py:582
  133.0 112.4 %collective-permute-start.10 = (bf16[2048,1024]{1,0:T(8,128)(2,1)}, bf16[2048,1024]{1,0:T(8,128)(2,1)}, u32[]{:S(2)}, u32[]{:S(2)}) collective-permute-start(bf16[2048,1024]{1,0:T(8,128)(2,1)} %get-tuple-element.279), channel_id=1, source_target_pairs={{0,2},{1,3},{2,0},{3,1},{4,6},{5,7},{6,4},{7,5}} | collective-permute-start | bytes 12582920 | tf_op jit(solution)/shard_map/ppermute | solution.py:582
  169.5 119.7 %collective-permute-start.9 = (bf16[2,2048,1024]{2,1,0:T(8,128)(2,1)}, bf16[2,2048,1024]{2,1,0:T(8,128)(2,1)}, u32[]{:S(2)}, u32[]{:S(2)}) collective-permute-start(bf16[2,2048,1024]{2,1,0:T(8,128)(2,1)} %refs_1_.49), channel_id=1, source_target_pairs={{0,1},{1,0},{2,3},{3,2},{4,5},{5,4},{6,7},{7,6}} | collective-permute-start | bytes 25165832 | tf_op jit(solution)/shard_map/ppermute | solution.py:586
  170.0 399.0 %collective-permute-start.14 = (bf16[2,1024,6144]{2,1,0:T(8,128)(2,1)}, bf16[2,1024,6144]{2,1,0:T(8,128)(2,1)}, u32[]{:S(2)}, u32[]{:S(2)}) collective-permute-start(bf16[2,1024,6144]{2,1,0:T(8,128)(2,1)} %refs_1_.61), channel_id=1, source_target_pairs={{0,1},{1,0},{2,3},{3,2},{4,5},{5,4},{6,7},{7,6}} | collective-permute-start | bytes 75497480 | tf_op jit(solution)/shard_map/ppermute | solution.py:586
  170.0 399.0 %collective-permute-start.15 = (bf16[2,1024,6144]{2,1,0:T(8,128)(2,1)}, bf16[2,1024,6144]{2,1,0:T(8,128)(2,1)}, u32[]{:S(2)}, u32[]{:S(2)}) collective-permute-start(bf16[2,1024,6144]{2,1,0:T(8,128)(2,1)} %refs_2_.39), channel_id=1, source_target_pairs={{0,1},{1,0},{2,3},{3,2},{4,5},{5,4},{6,7},{7,6}} | collective-permute-start | bytes 75497480 | tf_op jit(solution)/shard_map/ppermute | solution.py:586
  287.1 161.6 %collective-permute-start.16 = (bf16[1024,3584]{1,0:T(8,128)(2,1)}, bf16[1024,3584]{1,0:T(8,128)(2,1)}, u32[]{:S(2)}, u32[]{:S(2)}) collective-permute-start(bf16[1024,3584]{1,0:T(8,128)(2,1)} %pad_maximum_fusion), channel_id=1, source_target_pairs={{0,2},{1,3},{2,0},{3,1},{4,6},{5,7},{6,4},{7,5}} | collective-permute-start | bytes 22020104 | tf_op jit(solution)/shard_map/ppermute | solution.py:582
  303.1 153.5 %collective-permute-start.12 = (bf16[1024,2048]{1,0:T(8,128)(2,1)}, bf16[1024,2048]{1,0:T(8,128)(2,1)}, u32[]{:S(2)}, u32[]{:S(2)}) collective-permute-start(bf16[1024,2048]{1,0:T(8,128)(2,1)} %shard_map.125.refs_1_), channel_id=1, source_target_pairs={{0,4},{4,0},{1,5},{5,1},{2,6},{6,2},{3,7},{7,3}} | collective-permute-start | bytes 12582920 | tf_op jit(solution)/shard_map/ppermute | solution.py:588
  448.8 120.2 %collective-permute-start.17 = (bf16[1024,3584]{1,0:T(8,128)(2,1)}, bf16[1024,3584]{1,0:T(8,128)(2,1)}, u32[]{:S(2)}, u32[]{:S(2)}) collective-permute-start(bf16[1024,3584]{1,0:T(8,128)(2,1)} %collective-permute-done.16.refs_5_), channel_id=1, source_target_pairs={{0,1},{1,0},{2,3},{3,2},{4,5},{5,4},{6,7},{7,6}} | collective-permute-start | bytes 22020104 | tf_op jit(solution)/shard_map/ppermute | solution.py:584
  455.6 160.7 %collective-permute-start.18 = (bf16[1024,3584]{1,0:T(8,128)(2,1)}, bf16[1024,3584]{1,0:T(8,128)(2,1)}, u32[]{:S(2)}, u32[]{:S(2)}) collective-permute-start(bf16[1024,3584]{1,0:T(8,128)(2,1)} %pad_maximum_fusion.1), channel_id=1, source_target_pairs={{0,2},{1,3},{2,0},{3,1},{4,6},{5,7},{6,4},{7,5}} | collective-permute-start | bytes 22020104 | tf_op jit(solution)/shard_map/ppermute | solution.py:582
  456.6 92.7 %collective-permute-start.13 = (bf16[1024,2048]{1,0:T(8,128)(2,1)S(1)}, bf16[1024,2048]{1,0:T(8,128)(2,1)S(1)}, u32[]{:S(2)}, u32[]{:S(2)}) collective-permute-start(bf16[1024,2048]{1,0:T(8,128)(2,1)S(1)} %copy-done.4), channel_id=1, source_target_pairs={{0,4},{4,0},{1,5},{5,1},{2,6},{6,2},{3,7},{7,3}} | collective-permute-start | bytes 12582920 | tf_op jit(solution)/shard_map/ppermute | solution.py:588
  616.3 460.0 %collective-permute-start.28 = (bf16[2,6144,1024]{2,1,0:T(8,128)(2,1)}, bf16[2,6144,1024]{2,1,0:T(8,128)(2,1)}, u32[]{:S(2)}, u32[]{:S(2)}) collective-permute-start(bf16[2,6144,1024]{2,1,0:T(8,128)(2,1)} %refs_1_.63), channel_id=1, source_target_pairs={{0,1},{1,0},{2,3},{3,2},{4,5},{5,4},{6,7},{7,6}} | collective-permute-start | bytes 75497480 | tf_op jit(solution)/shard_map/ppermute | solution.py:586
  637.2 93.8 %collective-permute-start.21 = (bf16[1024,2048]{1,0:T(8,128)(2,1)}, bf16[1024,2048]{1,0:T(8,128)(2,1)}, u32[]{:S(2)}, u32[]{:S(2)}) collective-permute-start(bf16[1024,2048]{1,0:T(8,128)(2,1)} %shard_map.130.refs_2_), channel_id=1, source_target_pairs={{0,4},{4,0},{1,5},{5,1},{2,6},{6,2},{3,7},{7,3}} | collective-permute-start | bytes 12582920 | tf_op jit(solution)/shard_map/ppermute | solution.py:588
  638.2 181.6 %collective-permute-start.20 = (bf16[1024,2048]{1,0:T(8,128)(2,1)}, bf16[1024,2048]{1,0:T(8,128)(2,1)}, u32[]{:S(2)}, u32[]{:S(2)}) collective-permute-start(bf16[1024,2048]{1,0:T(8,128)(2,1)} %shard_map.129.refs_1_), channel_id=1, source_target_pairs={{0,4},{4,0},{1,5},{5,1},{2,6},{6,2},{3,7},{7,3}} | collective-permute-start | bytes 12582920 | tf_op jit(solution)/shard_map/ppermute | solution.py:588
  644.3 231.6 %collective-permute-start.22 = (bf16[1024,2560]{1,0:T(8,128)(2,1)}, bf16[1024,2560]{1,0:T(8,128)(2,1)}, u32[]{:S(2)}, u32[]{:S(2)}) collective-permute-start(bf16[1024,2560]{1,0:T(8,128)(2,1)} %pad_maximum_fusion.4), channel_id=1, source_target_pairs={{0,2},{1,3},{2,0},{3,1},{4,6},{5,7},{6,4},{7,5}} | collective-permute-start | bytes 15728648 | tf_op jit(solution)/shard_map/ppermute | solution.py:582
  1015.9 139.1 %collective-permute-start.29 = (bf16[6144,512]{1,0:T(8,128)(2,1)}, bf16[6144,512]{1,0:T(8,128)(2,1)}, u32[]{:S(2)}, u32[]{:S(2)}) collective-permute-start(bf16[6144,512]{1,0:T(8,128)(2,1)} %get-tuple-element.177), channel_id=1, source_target_pairs={{0,2},{1,3},{2,0},{3,1},{4,6},{5,7},{6,4},{7,5}} | collective-permute-start | bytes 18874376 | tf_op jit(solution)/shard_map/ppermute | solution.py:582
  1155.3 138.0 %collective-permute-start.31 = (bf16[6144,512]{1,0:T(8,128)(2,1)}, bf16[6144,512]{1,0:T(8,128)(2,1)}, u32[]{:S(2)}, u32[]{:S(2)}) collective-permute-start(bf16[6144,512]{1,0:T(8,128)(2,1)} %get-tuple-element.180), channel_id=1, source_target_pairs={{0,2},{1,3},{2,0},{3,1},{4,6},{5,7},{6,4},{7,5}} | collective-permute-start | bytes 18874376 | tf_op jit(solution)/shard_map/ppermute | solution.py:582
  1293.3 202.6 %collective-permute-start.39 = (bf16[1024,2048]{1,0:T(8,128)(2,1)}, bf16[1024,2048]{1,0:T(8,128)(2,1)}, u32[]{:S(2)}, u32[]{:S(2)}) collective-permute-start(bf16[1024,2048]{1,0:T(8,128)(2,1)} %slice_bitcast_fusion.7.refs_0_), channel_id=1, source_target_pairs={{0,2},{1,3},{2,0},{3,1},{4,6},{5,7},{6,4},{7,5}} | collective-permute-start | bytes 12582920 | tf_op jit(solution)/shard_map/ppermute | solution.py:582
  1295.1 182.1 %collective-permute-start.35 = (bf16[1024,1024]{1,0:T(8,128)(2,1)}, bf16[1024,1024]{1,0:T(8,128)(2,1)}, u32[]{:S(2)}, u32[]{:S(2)}) collective-permute-start(bf16[1024,1024]{1,0:T(8,128)(2,1)} %shard_map.143.refs_3_), channel_id=1, source_target_pairs={{0,4},{4,0},{1,5},{5,1},{2,6},{6,2},{3,7},{7,3}} | collective-permute-start | bytes 6291464 | tf_op jit(solution)/shard_map/ppermute | solution.py:588
  1296.3 181.9 %collective-permute-start.36 = (bf16[1024,1024]{1,0:T(8,128)(2,1)}, bf16[1024,1024]{1,0:T(8,128)(2,1)}, u32[]{:S(2)}, u32[]{:S(2)}) collective-permute-start(bf16[1024,1024]{1,0:T(8,128)(2,1)} %shard_map.149.refs_4_), channel_id=1, source_target_pairs={{0,4},{4,0},{1,5},{5,1},{2,6},{6,2},{3,7},{7,3}} | collective-permute-start | bytes 6291464 | tf_op jit(solution)/shard_map/ppermute | solution.py:588
  1323.1 155.1 %collective-permute-start.37 = (bf16[1024,1024]{1,0:T(8,128)(2,1)}, bf16[1024,1024]{1,0:T(8,128)(2,1)}, u32[]{:S(2)}, u32[]{:S(2)}) collective-permute-start(bf16[1024,1024]{1,0:T(8,128)(2,1)} %shard_map.150.refs_5_), channel_id=1, source_target_pairs={{0,4},{4,0},{1,5},{5,1},{2,6},{6,2},{3,7},{7,3}} | collective-permute-start | bytes 6291464 | tf_op jit(solution)/shard_map/ppermute | solution.py:588
  1344.0 133.2 %collective-permute-start.33 = (bf16[1024,512]{1,0:T(8,128)(2,1)S(1)}, bf16[1024,512]{1,0:T(8,128)(2,1)}, u32[]{:S(2)}, u32[]{:S(2)}) collective-permute-start(bf16[1024,512]{1,0:T(8,128)(2,1)S(1)} %copy-done.9), channel_id=1, source_target_pairs={{0,4},{4,0},{1,5},{5,1},{2,6},{6,2},{3,7},{7,3}} | collective-permute-start | bytes 3145736 | tf_op jit(solution)/shard_map/ppermute | solution.py:588
  1525.6 93.4 %collective-permute-start.49 = (bf16[2048,1024]{1,0:T(8,128)(2,1)}, bf16[2048,1024]{1,0:T(8,128)(2,1)}, u32[]{:S(2)}, u32[]{:S(2)}) collective-permute-start(bf16[2048,1024]{1,0:T(8,128)(2,1)} %get-tuple-element.201), channel_id=1, source_target_pairs={{0,2},{1,3},{2,0},{3,1},{4,6},{5,7},{6,4},{7,5}} | collective-permute-start | bytes 12582920 | tf_op jit(solution)/shard_map/ppermute | solution.py:582
  1619.0 202.0 %collective-permute-start.50 = (bf16[2048,1024]{1,0:T(8,128)(2,1)}, bf16[2048,1024]{1,0:T(8,128)(2,1)}, u32[]{:S(2)}, u32[]{:S(2)}) collective-permute-start(bf16[2048,1024]{1,0:T(8,128)(2,1)} %collective-permute-done.49.refs_1_), channel_id=1, source_target_pairs={{0,1},{1,0},{2,3},{3,2},{4,5},{5,4},{6,7},{7,6}} | collective-permute-start | bytes 12582920 | tf_op jit(solution)/shard_map/ppermute | solution.py:584
  1620.1 183.2 %collective-permute-start.46 = (bf16[1024,1024]{1,0:T(8,128)(2,1)}, bf16[1024,1024]{1,0:T(8,128)(2,1)}, u32[]{:S(2)}, u32[]{:S(2)}) collective-permute-start(bf16[1024,1024]{1,0:T(8,128)(2,1)} %shard_map.148.refs_3_), channel_id=1, source_target_pairs={{0,4},{4,0},{1,5},{5,1},{2,6},{6,2},{3,7},{7,3}} | collective-permute-start | bytes 6291464 | tf_op jit(solution)/shard_map/ppermute | solution.py:588
  1621.3 182.0 %collective-permute-start.48 = (bf16[1024,1024]{1,0:T(8,128)(2,1)}, bf16[1024,1024]{1,0:T(8,128)(2,1)}, u32[]{:S(2)}, u32[]{:S(2)}) collective-permute-start(bf16[1024,1024]{1,0:T(8,128)(2,1)} %shard_map.152.refs_5_), channel_id=1, source_target_pairs={{0,4},{4,0},{1,5},{5,1},{2,6},{6,2},{3,7},{7,3}} | collective-permute-start | bytes 6291464 | tf_op jit(solution)/shard_map/ppermute | solution.py:588
  1622.1 181.2 %collective-permute-start.47 = (bf16[1024,1024]{1,0:T(8,128)(2,1)}, bf16[1024,1024]{1,0:T(8,128)(2,1)}, u32[]{:S(2)}, u32[]{:S(2)}) collective-permute-start(bf16[1024,1024]{1,0:T(8,128)(2,1)} %shard_map.151.refs_4_), channel_id=1, source_target_pairs={{0,4},{4,0},{1,5},{5,1},{2,6},{6,2},{3,7},{7,3}} | collective-permute-start | bytes 6291464 | tf_op jit(solution)/shard_map/ppermute | solution.py:588
  1645.5 156.6 %collective-permute-start.44 = (bf16[1024,512]{1,0:T(8,128)(2,1)S(1)}, bf16[1024,512]{1,0:T(8,128)(2,1)S(1)}, u32[]{:S(2)}, u32[]{:S(2)}) collective-permute-start(bf16[1024,512]{1,0:T(8,128)(2,1)S(1)} %copy-done.8), channel_id=1, source_target_pairs={{0,4},{4,0},{1,5},{5,1},{2,6},{6,2},{3,7},{7,3}} | collective-permute-start | bytes 3145736 | tf_op jit(solution)/shard_map/ppermute | solution.py:588
  1802.1 163.4 %collective-permute-start.53 = (bf16[1024,3584]{1,0:T(8,128)(2,1)}, bf16[1024,3584]{1,0:T(8,128)(2,1)}, u32[]{:S(2)}, u32[]{:S(2)}) collective-permute-start(bf16[1024,3584]{1,0:T(8,128)(2,1)} %pad_maximum_fusion.2), channel_id=1, source_target_pairs={{0,2},{1,3},{2,0},{3,1},{4,6},{5,7},{6,4},{7,5}} | collective-permute-start | bytes 22020104 | tf_op jit(solution)/shard_map/ppermute | solution.py:582
  1965.5 210.1 %collective-permute-start.54 = (bf16[1024,3584]{1,0:T(8,128)(2,1)}, bf16[1024,3584]{1,0:T(8,128)(2,1)}, u32[]{:S(2)}, u32[]{:S(2)}) collective-permute-start(bf16[1024,3584]{1,0:T(8,128)(2,1)} %collective-permute-done.53.refs_5_), channel_id=1, source_target_pairs={{0,1},{1,0},{2,3},{3,2},{4,5},{5,4},{6,7},{7,6}} | collective-permute-start | bytes 22020104 | tf_op jit(solution)/shard_map/ppermute | solution.py:584
  1972.4 241.7 %collective-permute-start.55 = (bf16[1024,3584]{1,0:T(8,128)(2,1)}, bf16[1024,3584]{1,0:T(8,128)(2,1)}, u32[]{:S(2)}, u32[]{:S(2)}) collective-permute-start(bf16[1024,3584]{1,0:T(8,128)(2,1)} %pad_maximum_fusion.3), channel_id=1, source_target_pairs={{0,2},{1,3},{2,0},{3,1},{4,6},{5,7},{6,4},{7,5}} | collective-permute-start | bytes 22020104 | tf_op jit(solution)/shard_map/ppermute | solution.py:582
  1973.3 93.4 %collective-permute-start.51 = (bf16[1024,2048]{1,0:T(8,128)(2,1)S(1)}, bf16[1024,2048]{1,0:T(8,128)(2,1)S(1)}, u32[]{:S(2)}, u32[]{:S(2)}) collective-permute-start(bf16[1024,2048]{1,0:T(8,128)(2,1)S(1)} %copy-done.3), channel_id=1, source_target_pairs={{0,4},{4,0},{1,5},{5,1},{2,6},{6,2},{3,7},{7,3}} | collective-permute-start | bytes 12582920 | tf_op jit(solution)/shard_map/ppermute | solution.py:588
  1974.8 181.0 %collective-permute-start.52 = (bf16[1024,2048]{1,0:T(8,128)(2,1)}, bf16[1024,2048]{1,0:T(8,128)(2,1)S(1)}, u32[]{:S(2)}, u32[]{:S(2)}) collective-permute-start(bf16[1024,2048]{1,0:T(8,128)(2,1)} %shard_map.158.refs_2_), channel_id=1, source_target_pairs={{0,4},{4,0},{1,5},{5,1},{2,6},{6,2},{3,7},{7,3}} | collective-permute-start | bytes 12582920 | tf_op jit(solution)/shard_map/ppermute | solution.py:588
  2214.1 93.8 %collective-permute-start.58 = (bf16[1024,2048]{1,0:T(8,128)(2,1)}, bf16[1024,2048]{1,0:T(8,128)(2,1)}, u32[]{:S(2)}, u32[]{:S(2)}) collective-permute-start(bf16[1024,2048]{1,0:T(8,128)(2,1)} %shard_map.162.refs_2_), channel_id=1, source_target_pairs={{0,4},{4,0},{1,5},{5,1},{2,6},{6,2},{3,7},{7,3}} | collective-permute-start | bytes 12582920 | tf_op jit(solution)/shard_map/ppermute | solution.py:588
  2215.6 181.6 %collective-permute-start.57 = (bf16[1024,2048]{1,0:T(8,128)(2,1)}, bf16[1024,2048]{1,0:T(8,128)(2,1)}, u32[]{:S(2)}, u32[]{:S(2)}) collective-permute-start(bf16[1024,2048]{1,0:T(8,128)(2,1)} %shard_map.161.refs_1_), channel_id=1, source_target_pairs={{0,4},{4,0},{1,5},{5,1},{2,6},{6,2},{3,7},{7,3}} | collective-permute-start | bytes 12582920 | tf_op jit(solution)/shard_map/ppermute | solution.py:588
  2222.6 230.7 %collective-permute-start.59 = (bf16[1024,2560]{1,0:T(8,128)(2,1)}, bf16[1024,2560]{1,0:T(8,128)(2,1)}, u32[]{:S(2)}, u32[]{:S(2)}) collective-permute-start(bf16[1024,2560]{1,0:T(8,128)(2,1)} %pad_maximum_fusion.5), channel_id=1, source_target_pairs={{0,2},{1,3},{2,0},{3,1},{4,6},{5,7},{6,4},{7,5}} | collective-permute-start | bytes 15728648 | tf_op jit(solution)/shard_map/ppermute | solution.py:582
  2593.3 138.8 %collective-permute-start.65 = (bf16[6144,512]{1,0:T(8,128)(2,1)}, bf16[6144,512]{1,0:T(8,128)(2,1)}, u32[]{:S(2)}, u32[]{:S(2)}) collective-permute-start(bf16[6144,512]{1,0:T(8,128)(2,1)} %get-tuple-element.240), channel_id=1, source_target_pairs={{0,2},{1,3},{2,0},{3,1},{4,6},{5,7},{6,4},{7,5}} | collective-permute-start | bytes 18874376 | tf_op jit(solution)/shard_map/ppermute | solution.py:582
  2732.1 138.2 %collective-permute-start.67 = (bf16[6144,512]{1,0:T(8,128)(2,1)}, bf16[6144,512]{1,0:T(8,128)(2,1)}, u32[]{:S(2)}, u32[]{:S(2)}) collective-permute-start(bf16[6144,512]{1,0:T(8,128)(2,1)} %get-tuple-element.244), channel_id=1, source_target_pairs={{0,2},{1,3},{2,0},{3,1},{4,6},{5,7},{6,4},{7,5}} | collective-permute-start | bytes 18874376 | tf_op jit(solution)/shard_map/ppermute | solution.py:582
  2880.8 90.0 %collective-permute-start.70 = (bf16[1024,512]{1,0:T(8,128)(2,1)}, bf16[1024,512]{1,0:T(8,128)(2,1)}, u32[]{:S(2)}, u32[]{:S(2)}) collective-permute-start(bf16[1024,512]{1,0:T(8,128)(2,1)} %shard_map.178.p_ref), channel_id=1, source_target_pairs={{0,4},{4,0},{1,5},{5,1},{2,6},{6,2},{3,7},{7,3}} | collective-permute-start | bytes 3145736 | tf_op jit(solution)/shard_map/ppermute | solution.py:588
  2881.3 134.4 %collective-permute-start.73 = (bf16[1024,1024]{1,0:T(8,128)(2,1)}, bf16[1024,1024]{1,0:T(8,128)(2,1)}, u32[]{:S(2)}, u32[]{:S(2)}) collective-permute-start(bf16[1024,1024]{1,0:T(8,128)(2,1)} %shard_map.175.p_ref), channel_id=1, source_target_pairs={{0,4},{4,0},{1,5},{5,1},{2,6},{6,2},{3,7},{7,3}} | collective-permute-start | bytes 6291464 | tf_op jit(solution)/shard_map/ppermute | solution.py:588
  2921.5 139.1 %collective-permute-start.74 = (bf16[1024,1024]{1,0:T(8,128)(2,1)}, bf16[1024,1024]{1,0:T(8,128)(2,1)}, u32[]{:S(2)}, u32[]{:S(2)}) collective-permute-start(bf16[1024,1024]{1,0:T(8,128)(2,1)} %shard_map.180.p_ref), channel_id=1, source_target_pairs={{0,4},{4,0},{1,5},{5,1},{2,6},{6,2},{3,7},{7,3}} | collective-permute-start | bytes 6291464 | tf_op jit(solution)/shard_map/ppermute | solution.py:588
  2925.9 230.4 %collective-permute-start.76 = (bf16[1024,1024]{1,0:T(8,128)(2,1)}, bf16[1024,1024]{1,0:T(8,128)(2,1)}, u32[]{:S(2)}, u32[]{:S(2)}) collective-permute-start(bf16[1024,1024]{1,0:T(8,128)(2,1)} %shard_map.182.p_ref), channel_id=1, source_target_pairs={{0,4},{4,0},{1,5},{5,1},{2,6},{6,2},{3,7},{7,3}} | collective-permute-start | bytes 6291464 | tf_op jit(solution)/shard_map/ppermute | solution.py:588
  2948.3 202.2 %collective-permute-start.75 = (bf16[1024,1024]{1,0:T(8,128)(2,1)}, bf16[1024,1024]{1,0:T(8,128)(2,1)}, u32[]{:S(2)}, u32[]{:S(2)}) collective-permute-start(bf16[1024,1024]{1,0:T(8,128)(2,1)} %shard_map.181.p_ref), channel_id=1, source_target_pairs={{0,4},{4,0},{1,5},{5,1},{2,6},{6,2},{3,7},{7,3}} | collective-permute-start | bytes 6291464 | tf_op jit(solution)/shard_map/ppermute | solution.py:588
  2970.8 224.7 %collective-permute-start.77 = (bf16[1024,1024]{1,0:T(8,128)(2,1)}, bf16[1024,1024]{1,0:T(8,128)(2,1)}, u32[]{:S(2)}, u32[]{:S(2)}) collective-permute-start(bf16[1024,1024]{1,0:T(8,128)(2,1)} %shard_map.183.p_ref), channel_id=1, source_target_pairs={{0,4},{4,0},{1,5},{5,1},{2,6},{6,2},{3,7},{7,3}} | collective-permute-start | bytes 6291464 | tf_op jit(solution)/shard_map/ppermute | solution.py:588
  3015.7 224.2 %collective-permute-start.78 = (bf16[1024,1024]{1,0:T(8,128)(2,1)}, bf16[1024,1024]{1,0:T(8,128)(2,1)}, u32[]{:S(2)}, u32[]{:S(2)}) collective-permute-start(bf16[1024,1024]{1,0:T(8,128)(2,1)} %shard_map.184.p_ref), channel_id=1, source_target_pairs={{0,4},{4,0},{1,5},{5,1},{2,6},{6,2},{3,7},{7,3}} | collective-permute-start | bytes 6291464 | tf_op jit(solution)/shard_map/ppermute | solution.py:588
  (51 other events, 1455.0 us)
